TPU v7x, 32 devices: a whole 2x2x4 slice. The times are simulated.
32 devices in a mesh: blk: 8 (over z, y), grid: 4 (over x, core).
Axes of the slice: x: 2, y: 2, z: 4, core: 2. Of those that a mesh axis runs over, the one named last changes fastest.
Arguments:
- orbitals: bfloat16 [32, 64, 4096], P('blk', 'grid'), may hold values from -60 to 60
Outputs:
- rotated: bfloat16 [32, 64, 4096], P(None, 'grid', 'blk')
- intersection: float32 [32, 32], replicated
All inputs are finite; a program needn't handle non-finite values.
Results may differ from a plain program's by a relative error of at most 0.0085.
Values may be sent and summed in bfloat16 or wider, within the bound.
No kernel may reach another device: no remote copies, remote signals or barrier semaphores. Data moves between devices by JAX's collectives and lax.ppermute only.
A program may use at most 128 MiB of HBM per device.

v0:
```python
import functools

import jax
import jax.numpy as jnp
from jax import lax
from jax.experimental import pallas as pl
from jax.experimental.pallas import tpu as pltpu
from jax.sharding import PartitionSpec as P


NX = 64
NY = 64
NZ = 64
STEPS = 2

exchange_fraction = 0.25
screening = 1.0

BF = jnp.bfloat16
F32 = jnp.float32
VMEM = pl.BlockSpec(memory_space=pltpu.VMEM)
SMEM = pl.BlockSpec(memory_space=pltpu.SMEM)
LANES = 128
ROW_PAD = 1
SMALL_VMEM = 10 * 1024 * 1024
QUAD = 4
PANEL = 8


def product(a, b):
    return jnp.dot(a, b, preferred_element_type=F32)


def sines(rows, columns, length):
    angle = jnp.pi * (rows + 1.0) * (columns + 1.0) / (length + 1)
    return jnp.sqrt(2.0 / (length + 1)) * jnp.sin(angle)


def eigen_values(index, length):
    return 2.0 - 2.0 * jnp.cos(jnp.pi * (index + 1.0) / (length + 1))


def table_kernel(slab_rows, diag_ref, weight_ref):
    size = diag_ref.shape[1]
    copies = size // NX
    grid_index = lax.axis_index("grid")

    def cells_of(position):
        slab = position // slab_rows
        start = jnp.zeros_like(position)
        for r in range(NX // slab_rows):
            start = jnp.where(slab == r, (grid_index ^ r) * slab_rows, start)
        return start + position % slab_rows

    shape = (NX, LANES)
    down = lax.broadcasted_iota(jnp.int32, shape, 0)
    along = lax.broadcasted_iota(jnp.int32, shape, 1) % NX
    pairs = (
        (down, along),
        (down, cells_of(along)),
        (cells_of(down), along),
    )
    same = (
        lax.broadcasted_iota(jnp.int32, (NX, size), 1) // NX
    )
    for i, (row, column) in enumerate(pairs):
        table = sines(row.astype(F32), column.astype(F32), NX)
        table = jnp.concatenate([table] * (size // LANES), 1)
        for c in range(copies):
            block = jnp.where(same == c, table, 0.0).astype(BF)
            diag_ref[i, c * NX:(c + 1) * NX, :] = block
            if i == 0:
                block = (block.astype(F32) * exchange_fraction).astype(BF)
                diag_ref[len(pairs), c * NX:(c + 1) * NX, :] = block
    lam = eigen_values(down.astype(F32), NX)
    plane = screening + lam + eigen_values(along.astype(F32), NZ)
    for k in range(NX):
        weight_ref[k * NY:(k + 1) * NY, :] = 1.0 / (lam[k:k + 1, :] + plane)


def make_tables(slab_rows):
    size = QUAD * NX
    return pl.pallas_call(
        functools.partial(table_kernel, slab_rows),
        out_shape=(
            jax.ShapeDtypeStruct((4, size, size), BF),
            jax.ShapeDtypeStruct((NX * NY, LANES), F32),
        ),
        out_specs=(VMEM, VMEM),
        compiler_params=pltpu.CompilerParams(vmem_limit_bytes=SMALL_VMEM),
        cost_estimate=pl.CostEstimate(flops=1 << 28, bytes_accessed=3 << 20, transcendentals=0),
    )()


def rows_of(refs):
    return [(ref, j) for ref in refs for j in range(ref.shape[0])]


def block_kernel(counts, final, rest):
    grid_index = lax.axis_index("grid")
    core, chip = grid_index % 2, grid_index // 2
    refs, rest = list(rest[:sum(counts)]), rest[sum(counts):]
    local, passed, src = [
        [refs.pop(0) for _ in range(count)] for count in counts
    ]
    local, passed, src = rows_of(local), rows_of(passed), rows_of(src)
    tab_ref, w_ref = rest[:2]
    rest = rest[2:]
    if final:
        acc_ref, keep_ref, send_ref, grouped_ref, work_ref = rest
    else:
        out_ref, grouped_ref, work_ref = rest
    owns = len(local) // (NX // local[0][0].shape[1])
    count = len(src) // (NX // src[0][0].shape[1])
    halves = owns * count * NZ // LANES
    pitch = work_ref.shape[1] // NY

    low = lax.broadcasted_iota(jnp.int32, (NX, LANES), 1) < NZ
    low16 = lax.broadcasted_iota(jnp.int16, (NX, LANES), 1) < NZ

    def swapped(x):
        return jnp.concatenate([x[:, NZ:], x[:, :NZ]], 1)

    def tile(rows, j, off):
        return jnp.concatenate(
            [ref[at, :, pl.ds(off, LANES)] for ref, at in rows[j::count]], 0)

    def picked(rows, o, off):
        turn = (core + o) % owns
        return jnp.concatenate(
            [ref[at + turn, :, pl.ds(off, LANES)] for ref, at in rows[::owns]], 0)

    def own_tile(o, off):
        return jnp.where(core == chip, picked(local, o, off), picked(passed, o, off))

    def forward(t):
        at = t * QUAD * NX
        rows_d, rows_s = [], []
        for q in range(0, QUAD, LANES // NZ):
            off = (t * QUAD + q) * NZ
            a, b = tile(src, 0, off), tile(src, 1, off)
            mixed = swapped(jnp.where(low16, b, a))
            pair = [jnp.where(low16, a, mixed), jnp.where(low16, mixed, b)]
            rows_s += pair
            wide = []
            for o in range(owns):
                mine = own_tile(o, off)
                turned = swapped(mine)
                wide.append([jnp.where(low16, mine, turned), jnp.where(low16, turned, mine)])
            for y in range(2):
                rows_d.append(jnp.concatenate([w[y] * pair[y] for w in wide], 1))
        grouped_ref[pl.ds(at, QUAD * NX), :] = jnp.concatenate(rows_s, 0)
        first = product(jnp.concatenate(rows_d, 0), tab_ref[0]).astype(BF)
        modes = product(tab_ref[1], first)
        for q in range(QUAD):
            to = (t * QUAD + q) * pitch
            for h in range(halves):
                work_ref[h, pl.ds(to, NX), :] = modes[q * NX:(q + 1) * NX, h * LANES:(h + 1) * LANES]

    def solve(t):
        at = t * QUAD * NY
        modes = jnp.concatenate([
            jnp.concatenate(
                [work_ref[h, pl.ds(t * QUAD + q, NY, stride=pitch), :] for h in range(halves)], 1)
            for q in range(QUAD)], 0).astype(BF)
        weights = jnp.concatenate([w_ref[pl.ds(at, QUAD * NY), :]] * halves, 1)
        scaled = (product(tab_ref[0], modes) * weights).astype(BF)
        back = product(tab_ref[0], scaled)
        for q in range(QUAD):
            for h in range(halves):
                work_ref[h, pl.ds(t * QUAD + q, NY, stride=pitch), :] = (
                    back[q * NY:(q + 1) * NY, h * LANES:(h + 1) * LANES])

    def backward(t):
        at = t * QUAD * NX
        modes = jnp.concatenate([
            jnp.concatenate(
                [work_ref[h, pl.ds((t * QUAD + q) * pitch, NX), :] for h in range(halves)], 1)
            for q in range(QUAD)], 0).astype(BF)
        third = product(tab_ref[2], modes).astype(BF)
        potential = product(third, tab_ref[3])
        for q in range(0, QUAD, LANES // NZ):
            off = (t * QUAD + q) * NZ
            factor = [
                grouped_ref[pl.ds(at + (q + y) * NX, NX), :].astype(F32) for y in range(2)
            ]
            for o in range(owns):
                a, b = [
                    potential[(q + y) * NX:(q + y + 1) * NX, o * LANES:(o + 1) * LANES] * factor[y]
                    for y in range(2)
                ]
                exchange = jnp.where(low, a, b) + pltpu.roll(jnp.where(low, b, a), NZ, 1)
                if not final:
                    out_ref[o, :, pl.ds(off, LANES)] = exchange
                    continue
                exchange = exchange + acc_ref[o, :, pl.ds(off, LANES)]
                if o == 0:
                    keep_ref[:, pl.ds(off, LANES)] = own_tile(0, off).astype(F32) - exchange
                else:
                    send_ref[:, pl.ds(off, LANES)] = exchange.astype(send_ref.dtype)

    for step, trips in ((forward, NY // QUAD), (solve, NX // QUAD), (backward, NY // QUAD)):
        for t in range(trips):
            step(t)


def add_block(local, passed, src, tables, acc):
    owns, rows, cells = local[0].shape
    count = sum(x.shape[0] for x in src) * rows // NX
    assert count * NZ == LANES and owns == 2
    counts = (len(local), len(passed), len(src))
    final = acc is not None
    lead = () if acc is None else (acc,)
    flops = 12 * owns * count * NX * NY * NZ * NZ * 4
    if final:
        out_shape = (
            jax.ShapeDtypeStruct((NX, cells), F32), jax.ShapeDtypeStruct((NX, cells), BF))
    else:
        out_shape = jax.ShapeDtypeStruct((owns, NX, cells), F32)
    return pl.pallas_call(
        lambda *refs: block_kernel(counts, final, refs),
        out_shape=out_shape,
        in_specs=[VMEM] * (sum(counts) + 2 + len(lead)),
        out_specs=(VMEM, VMEM) if final else VMEM,
        scratch_shapes=[
            pltpu.VMEM((NY * NX, count * NZ), BF),
            pltpu.VMEM((owns * count * NZ // LANES, NY * (NX + ROW_PAD), LANES), F32),
        ],
        compiler_params=pltpu.CompilerParams(vmem_limit_bytes=24 * 1024 * 1024),
        cost_estimate=pl.CostEstimate(flops=flops, bytes_accessed=8 << 20, transcendentals=0),
    )(*local, *passed, *src, *tables, *lead)


def combine_kernel(slabs, keep_ref, part_ref, out_ref):
    grid_index = lax.axis_index("grid")
    rows = keep_ref.shape[0] // slabs
    for r in range(slabs):
        other = (r ^ 1) * rows
        updated = keep_ref[r * rows:(r + 1) * rows] - part_ref[other:other + rows].astype(F32)
        updated = updated.astype(BF)
        if len(out_ref.shape) == 3:
            out_ref[grid_index ^ r] = updated
            continue
        share = out_ref.shape[3]
        for b in range(out_ref.shape[0]):
            out_ref[b, grid_index ^ r] = updated[:, b * share:(b + 1) * share]


def gram_kernel(x_ref, out_ref):
    orbs, rows, lanes = x_ref.shape
    flat = x_ref[...].reshape(orbs * rows, lanes)
    full = lax.dot_general(flat, flat, (((1,), (1,)), ((), ())), preferred_element_type=F32)
    down = lax.broadcasted_iota(jnp.int32, (rows, orbs * rows), 0)
    along = lax.broadcasted_iota(jnp.int32, (rows, orbs * rows), 1)
    same = down == along % rows
    half = [
        jnp.sum(jnp.where(same, full[o * rows:(o + 1) * rows], 0.0), axis=0, keepdims=True)
        for o in range(orbs)
    ]
    half = jnp.concatenate(half, 0)
    gram = jnp.sum(half.T.reshape(orbs, rows, orbs), axis=1)
    deep = orbs * orbs // LANES
    packed = jnp.concatenate([gram[q * deep:(q + 1) * deep] for q in range(orbs // deep)], 1)
    out_ref[...] = jnp.broadcast_to(packed[None], out_ref.shape)


def rotate_kernel(scale, parts_ref, x_ref, out_ref, gram_ref):
    orbs, rows, lanes = x_ref.shape
    packed = jnp.sum(parts_ref[...], axis=0) * scale
    gram = jnp.concatenate(
        [packed[:, q * orbs:(q + 1) * orbs] for q in range(LANES // orbs)], 0)
    gram_ref[...] = gram
    down = lax.broadcasted_iota(jnp.int32, (orbs, orbs), 0)
    along = lax.broadcasted_iota(jnp.int32, (orbs, orbs), 1)
    eye = jnp.where(down == along, 1.0, 0.0)
    zero = jnp.zeros((orbs, LANES - 2 * orbs), F32)
    work = jnp.concatenate([gram, eye, zero], 1)
    row = lax.broadcasted_iota(jnp.int32, (orbs, LANES), 0)
    pivots = jnp.zeros((orbs, LANES), F32)
    for first in range(0, orbs, PANEL):
        columns = [
            jnp.broadcast_to(work[:, c:c + 1], (orbs, LANES)) for c in range(first, first + PANEL)
        ]
        for k in range(first, first + PANEL):
            column = columns[k - first]
            pivot = column[k:k + 1, :]
            pivots = jnp.where(row == k, pivot, pivots)
            factor = jnp.where(row > k, column * (1.0 / pivot), 0.0)
            work = work - factor * work[k:k + 1, :]
            for c in range(k - first + 1, PANEL):
                columns[c] = columns[c] - factor * columns[c][k:k + 1, :]
    work = work * (1.0 / jnp.sqrt(pivots))
    inverse = work[:, orbs:2 * orbs].astype(BF)
    tall = lax.broadcasted_iota(jnp.int32, (orbs * rows, orbs), 0) // rows
    wide = lax.broadcasted_iota(jnp.int32, (orbs * rows, orbs), 1)
    pick = jnp.where(tall == wide, 1.0, 0.0).astype(BF)
    spread = product(pick, inverse).astype(BF)
    spread = lax.dot_general(spread, pick, (((1,), (1,)), ((), ())), preferred_element_type=F32)
    i = lax.broadcasted_iota(jnp.int32, (orbs * rows, 1), 0) % rows
    j = lax.broadcasted_iota(jnp.int32, (1, orbs * rows), 1) % rows
    spread = jnp.where(i == j, spread, 0.0).astype(BF)
    flat = x_ref[...].reshape(orbs * rows, lanes)
    out_ref[...] = product(spread, flat).astype(BF).reshape(orbs, rows, lanes)


def exchanged(x, axis, by, only=None):
    return lax.ppermute(x, axis, [
        (i, i ^ by) for i in range(lax.axis_size(axis)) if only is None or only(i)])


def body(orbitals):
    orb_count, slab_rows, plane_cells = orbitals.shape
    slabs = lax.axis_size("grid")
    blocks = lax.axis_size("blk")
    assert orb_count == slabs == 4 and slab_rows * slabs == NX and blocks % 2 == 0 and STEPS == 2
    top = slabs // 2
    half = orb_count // 2
    core = lax.axis_index("grid") % 2
    even = lax.axis_index("blk") % 2 == 0
    diagonals, weights = make_tables(slab_rows)

    def shifted(x):
        return lax.ppermute(x, "blk", [(i, (i + 2) % blocks) for i in range(blocks)])

    def relayed(mine, received):
        relay = jnp.where(even, mine, received)
        return exchanged(relay, "blk", 1)

    def passed_on(x):
        return exchanged(x, "grid", 1, lambda i: i // 2 == i % 2)

    keep = lax.dynamic_slice_in_dim(orbitals, core * half, half, 0)
    give = lax.dynamic_slice_in_dim(orbitals, (1 - core) * half, half, 0)
    keep, give = lax.optimization_barrier((keep, give))
    held = [keep, exchanged(give, "grid", 1)]
    pieces = [held[0]] + list(lax.optimization_barrier(
        tuple(held[1][j:j + 1] for j in range(half))))
    far = [shifted(piece) for piece in pieces]
    across = [exchanged(held[i], "grid", top) for i in range(2)]
    near = [relayed(piece, far[i]) for i, piece in enumerate(pieces)]
    far_other = [shifted(across[0])] + [
        exchanged(far[i], "grid", top) for i in range(1, len(far))]
    relay, diagonals, weights = lax.optimization_barrier((across[0], diagonals, weights))
    tables = (diagonals, weights)
    near_other = [relayed(relay, far_other[0])] + [
        exchanged(near[i], "grid", top) for i in range(1, len(near))]
    local = held + across
    passed = [give, passed_on(held[0]), passed_on(jnp.concatenate([across[1], across[0]], 0))]
    acc = add_block(local, passed, far + far_other, tables, None)
    mine, other = add_block(local, passed, near + near_other, tables, acc)
    other = exchanged(other, "grid", 1)
    chunk = plane_cells // blocks
    if chunk % LANES == 0:
        shape = (blocks, slabs, slab_rows, chunk)
    else:
        shape = (slabs, slab_rows, plane_cells)
    updated = pl.pallas_call(
        functools.partial(combine_kernel, slabs),
        out_shape=jax.ShapeDtypeStruct(shape, BF),
        in_specs=[VMEM, VMEM],
        out_specs=VMEM,
        compiler_params=pltpu.CompilerParams(vmem_limit_bytes=SMALL_VMEM),
    )(mine, other)
    if chunk % LANES:
        updated = updated.reshape(slabs, slab_rows, blocks, chunk).transpose(2, 0, 1, 3)
    updated = updated.reshape(blocks * slabs, slab_rows, chunk)
    cellwise = lax.all_to_all(updated, ("blk", "grid"), 0, 0, tiled=True)

    devices = blocks * slabs
    cell_count = NX * NY * NZ
    if devices * slab_rows <= 512 and devices % PANEL == 0 and chunk % LANES == 0:
        local = pl.pallas_call(
            gram_kernel,
            out_shape=jax.ShapeDtypeStruct((devices, devices * devices // LANES, LANES), F32),
            in_specs=[VMEM],
            out_specs=VMEM,
            compiler_params=pltpu.CompilerParams(vmem_limit_bytes=SMALL_VMEM),
        )(cellwise)
        parts = lax.all_to_all(local, ("blk", "grid"), 0, 0, tiled=True)
        return pl.pallas_call(
            functools.partial(rotate_kernel, 1.0 / cell_count),
            out_shape=(
                jax.ShapeDtypeStruct(cellwise.shape, BF),
                jax.ShapeDtypeStruct((devices, devices), F32),
            ),
            in_specs=[VMEM, VMEM],
            out_specs=(VMEM, VMEM),
            compiler_params=pltpu.CompilerParams(vmem_limit_bytes=SMALL_VMEM),
        )(parts, cellwise)
    flat = cellwise.reshape(devices, slab_rows * chunk)
    local = jnp.dot(flat, flat.T, preferred_element_type=F32)
    intersection = lax.psum(local, ("blk", "grid")) / cell_count
    factor = jnp.linalg.cholesky(intersection)
    identity = jnp.eye(devices, dtype=F32)
    inverse = jax.scipy.linalg.solve_triangular(factor, identity, lower=True).astype(BF)
    rotated = product(inverse, flat).astype(BF)
    return (rotated.reshape(cellwise.shape), intersection)


def solution(mesh):
    in_specs = (P("blk", "grid", None),)
    out_specs = (P(None, "grid", "blk"), P())
    return jax.shard_map(body, mesh=mesh, in_specs=in_specs, out_specs=out_specs, check_vma=False)
```

profile of v0, /device:TPU:0, one launch (start us, length us, event | category | flops | bytes accessed | tf_op | source)
XLA Modules:
  0.0 82.8 jit_solution(11385497681822559191)
XLA Ops:
  0.6 1.1 %constant_dynamic-slice_fusion = (bf16[2,16,4096]{2,1,0:T(8,128)(2,1)S(1)}, bf16[2,16,4096]{2,1,0:T(8,128)(2,1)S(1)}) fusion(bf16[4,16,4096]{2,1,0:T(8,128)(2,1)} %param.1, s32[]{:T(128)S(6)} %select_n.43, s32[]{:T(128)S(6)} %select_n.42), kind=kLoop, calls=%fused_computation.5 | loop fusion | bytes 1048584 | tf_op jit(solution)/shard_map/dynamic_slice | solution.py:333
  1.7 0.6 collective-permute-start
  2.3 2.6 %collective-permute-start.5 = (bf16[2,16,4096]{2,1,0:T(8,128)(2,1)S(1)}, bf16[2,16,4096]{2,1,0:T(8,128)(2,1)S(1)}, u32[]{:S(2)}, u32[]{:S(2)}) collective-permute-start(bf16[2,16,4096]{2,1,0:T(8,128)(2,1)S(1)} %get-tuple-element.13.refs_0_), channel_id=1, source_target_pairs={{0,8},{4,12},{8,16},{12,20},{16,24},{20,28},{24,0},{28,4},{1,9},{5... | collective-permute-start | bytes 786440 | tf_op jit(solution)/shard_map/ppermute | solution.py:323
  4.9 2.1 %collective-permute-start.3 = (bf16[2,16,4096]{2,1,0:T(8,128)(2,1)S(1)}, bf16[2,16,4096]{2,1,0:T(8,128)(2,1)S(1)}, u32[]{:S(2)}, u32[]{:S(2)}) collective-permute-start(bf16[2,16,4096]{2,1,0:T(8,128)(2,1)S(1)} %get-tuple-element.13.refs_0_), channel_id=1, source_target_pairs={{0,1},{3,2},{4,5},{7,6},{8,9},{11,10},{12,13},{15,14},{16,17},{19,... | collective-permute-start | bytes 786440 | tf_op jit(solution)/shard_map/ppermute | solution.py:307
  7.0 0.8 collective-permute-start.1
  7.8 0.8 shard_map.30
  8.6 0.0 collective-permute-done.refs_1_
  8.6 1.6 %collective-permute-start.7 = (bf16[1,16,4096]{2,1,0:T(8,128)(2,1)S(1)}, bf16[1,16,4096]{2,1,0:T(8,128)(2,1)S(1)}, u32[]{:S(2)}, u32[]{:S(2)}) collective-permute-start(bf16[1,16,4096]{2,1,0:T(8,128)(2,1)S(1)} %get-tuple-element.15), channel_id=1, source_target_pairs={{0,8},{4,12},{8,16},{12,20},{16,24},{20,28},{24,0},{28,4},{1,9},{5... | collective-permute-start | bytes 393224 | tf_op jit(solution)/shard_map/ppermute | solution.py:323
  10.2 1.6 %collective-permute-start.9 = (bf16[1,16,4096]{2,1,0:T(8,128)(2,1)S(1)}, bf16[1,16,4096]{2,1,0:T(8,128)(2,1)S(1)}, u32[]{:S(2)}, u32[]{:S(2)}) collective-permute-start(bf16[1,16,4096]{2,1,0:T(8,128)(2,1)S(1)} %get-tuple-element.16), channel_id=1, source_target_pairs={{0,8},{4,12},{8,16},{12,20},{16,24},{20,28},{24,0},{28,4},{1,9},{5... | collective-permute-start | bytes 393224 | tf_op jit(solution)/shard_map/ppermute | solution.py:323
  11.8 3.6 %collective-permute-done.1.refs_2_ = bf16[2,16,4096]{2,1,0:T(8,128)(2,1)S(1)} collective-permute-done((bf16[2,16,4096]{2,1,0:T(8,128)(2,1)S(1)}, bf16[2,16,4096]{2,1,0:T(8,128)(2,1)S(1)}, u32[]{:S(2)}, u32[]{:S(2)}) %collective-permute-start.1) | collective-permute-done | bytes 262176 | tf_op jit(solution)/shard_map/ppermute | solution.py:307
  15.4 1.4 %collective-permute-start.2 = (bf16[2,16,4096]{2,1,0:T(8,128)(2,1)S(1)}, bf16[2,16,4096]{2,1,0:T(8,128)(2,1)S(1)}, u32[]{:S(2)}, u32[]{:S(2)}) collective-permute-start(bf16[2,16,4096]{2,1,0:T(8,128)(2,1)S(1)} %collective-permute-done.refs_1_), channel_id=1, source_target_pairs={{0,2},{1,3},{2,0},{3,1},{4,6},{5,7},{6,4},{7,5},{8,10},{9,11},{10,... | collective-permute-start | bytes 786440 | tf_op jit(solution)/shard_map/ppermute | solution.py:307
  16.8 0.0 collective-permute-done.5.refs_7_
  16.8 1.6 %collective-permute-start.11 = (bf16[2,16,4096]{2,1,0:T(8,128)(2,1)S(1)}, bf16[2,16,4096]{2,1,0:T(8,128)(2,1)S(1)}, u32[]{:S(2)}, u32[]{:S(2)}) collective-permute-start(bf16[2,16,4096]{2,1,0:T(8,128)(2,1)S(1)} %collective-permute-done.1.refs_2_), channel_id=1, source_target_pairs={{0,8},{4,12},{8,16},{12,20},{16,24},{20,28},{24,0},{28,4},{1,9},{5... | collective-permute-start | bytes 786440 | tf_op jit(solution)/shard_map/ppermute | solution.py:323
  18.4 0.0 collective-permute-done.7.refs_8_
  18.4 1.6 %collective-permute-start.8 = (bf16[1,16,4096]{2,1,0:T(8,128)(2,1)S(1)}, bf16[1,16,4096]{2,1,0:T(8,128)(2,1)S(1)}, u32[]{:S(2)}, u32[]{:S(2)}) collective-permute-start(bf16[1,16,4096]{2,1,0:T(8,128)(2,1)S(1)} %broadcast_select_fusion.3), channel_id=1, source_target_pairs={{0,4},{4,0},{8,12},{12,8},{16,20},{20,16},{24,28},{28,24},{1,5},{5... | collective-permute-start | bytes 393224 | tf_op jit(solution)/shard_map/ppermute | solution.py:307
  20.0 0.0 collective-permute-done.9.refs_9_
  20.0 1.1 %collective-permute-start.10 = (bf16[1,16,4096]{2,1,0:T(8,128)(2,1)S(1)}, bf16[1,16,4096]{2,1,0:T(8,128)(2,1)S(1)}, u32[]{:S(2)}, u32[]{:S(2)}) collective-permute-start(bf16[1,16,4096]{2,1,0:T(8,128)(2,1)S(1)} %broadcast_select_fusion.2), channel_id=1, source_target_pairs={{0,4},{4,0},{8,12},{12,8},{16,20},{20,16},{24,28},{28,24},{1,5},{5... | collective-permute-start | bytes 393224 | tf_op jit(solution)/shard_map/ppermute | solution.py:307
  21.1 2.4 %collective-permute-done.2.refs_3_ = bf16[2,16,4096]{2,1,0:T(8,128)(2,1)S(1)} collective-permute-done((bf16[2,16,4096]{2,1,0:T(8,128)(2,1)S(1)}, bf16[2,16,4096]{2,1,0:T(8,128)(2,1)S(1)}, u32[]{:S(2)}, u32[]{:S(2)}) %collective-permute-start.2) | collective-permute-done | bytes 262176 | tf_op jit(solution)/shard_map/ppermute | solution.py:307
  23.5 1.7 %collective-permute-start.15 = (bf16[1,16,4096]{2,1,0:T(8,128)(2,1)S(1)}, bf16[1,16,4096]{2,1,0:T(8,128)(2,1)S(1)}, u32[]{:S(2)}, u32[]{:S(2)}) collective-permute-start(bf16[1,16,4096]{2,1,0:T(8,128)(2,1)S(1)} %collective-permute-done.7.refs_8_), channel_id=1, source_target_pairs={{0,2},{1,3},{2,0},{3,1},{4,6},{5,7},{6,4},{7,5},{8,10},{9,11},{10,... | collective-permute-start | bytes 393224 | tf_op jit(solution)/shard_map/ppermute | solution.py:307
  25.3 0.0 collective-permute-done.3.refs_5_
  25.3 0.3 collective-permute-start.16
  25.7 1.1 %collective-permute-done.11.refs_10_ = bf16[2,16,4096]{2,1,0:T(8,128)(2,1)S(1)} collective-permute-done((bf16[2,16,4096]{2,1,0:T(8,128)(2,1)S(1)}, bf16[2,16,4096]{2,1,0:T(8,128)(2,1)S(1)}, u32[]{:S(2)}, u32[]{:S(2)}) %collective-permute-start.11) | collective-permute-done | bytes 262176 | tf_op jit(solution)/shard_map/ppermute | solution.py:323
  26.8 1.3 %collective-permute-start.4 = (bf16[4,16,4096]{2,1,0:T(8,128)(2,1)S(1)}, bf16[4,16,4096]{2,1,0:T(8,128)(2,1)S(1)}, u32[]{:S(2)}, u32[]{:S(2)}) collective-permute-start(bf16[4,16,4096]{2,1,0:T(8,128)(2,1)S(1)} %pad_maximum_fusion), channel_id=1, source_target_pairs={{0,1},{3,2},{4,5},{7,6},{8,9},{11,10},{12,13},{15,14},{16,17},{19,... | collective-permute-start | bytes 1572872 | tf_op jit(solution)/shard_map/ppermute | solution.py:307
  28.1 0.0 collective-permute-done.8.refs_8_
  28.1 1.6 %collective-permute-start.6 = (bf16[2,16,4096]{2,1,0:T(8,128)(2,1)S(1)}, bf16[2,16,4096]{2,1,0:T(8,128)(2,1)S(1)}, u32[]{:S(2)}, u32[]{:S(2)}) collective-permute-start(bf16[2,16,4096]{2,1,0:T(8,128)(2,1)S(1)} %broadcast_select_fusion.1), channel_id=1, source_target_pairs={{0,4},{4,0},{8,12},{12,8},{16,20},{20,16},{24,28},{28,24},{1,5},{5... | collective-permute-start | bytes 786440 | tf_op jit(solution)/shard_map/ppermute | solution.py:307
  29.7 0.1 collective-permute-done.15.refs_11_
  29.8 1.5 %collective-permute-start.12 = (bf16[2,16,4096]{2,1,0:T(8,128)(2,1)S(1)}, bf16[2,16,4096]{2,1,0:T(8,128)(2,1)S(1)}, u32[]{:S(2)}, u32[]{:S(2)}) collective-permute-start(bf16[2,16,4096]{2,1,0:T(8,128)(2,1)S(1)} %broadcast_select_fusion), channel_id=1, source_target_pairs={{0,4},{4,0},{8,12},{12,8},{16,20},{20,16},{24,28},{28,24},{1,5},{5... | collective-permute-start | bytes 786440 | tf_op jit(solution)/shard_map/ppermute | solution.py:307
  31.4 0.0 collective-permute-done.10.refs_9_
  31.4 1.7 %collective-permute-start.13 = (bf16[1,16,4096]{2,1,0:T(8,128)(2,1)S(1)}, bf16[1,16,4096]{2,1,0:T(8,128)(2,1)S(1)}, u32[]{:S(2)}, u32[]{:S(2)}) collective-permute-start(bf16[1,16,4096]{2,1,0:T(8,128)(2,1)S(1)} %collective-permute-done.8.refs_8_), channel_id=1, source_target_pairs={{0,2},{1,3},{2,0},{3,1},{4,6},{5,7},{6,4},{7,5},{8,10},{9,11},{10,... | collective-permute-start | bytes 393224 | tf_op jit(solution)/shard_map/ppermute | solution.py:307
  33.0 0.0 collective-permute-done.16.refs_12_
  33.0 0.4 collective-permute-start.14
  33.4 0.0 collective-permute-done.4.refs_6_
  33.4 4.4 %shard_map.31.refs_15_ = f32[2,64,4096]{2,1,0:T(8,128)S(1)} custom-call(bf16[2,16,4096]{2,1,0:T(8,128)(2,1)S(1)} %get-tuple-element.13.refs_0_, bf16[2,16,4096]{2,1,0:T(8,128)(2,1)S(1)} %collective-permute-done.refs_1_, bf16[2,16,4096]{2,1,0:T(8,128)(2,1)S(1)} %collective-permute-done.1.refs_2_, bf16[2,16,4096]{2,1,0:T(8,128)(2,1)S(1)} %collective-permute-done.2.refs_3_, ...), custom_call_target="tpu_custom_call" | custom-call | flops 3221225472 | bytes 8388608 | tf_op jit(solution)/shard_map/pallas_call | solution.py:220
  37.8 0.0 collective-permute-done.6.refs_7_
  37.8 0.0 collective-permute-done.13.refs_11_
  37.8 0.2 collective-permute-done.14.refs_12_
  38.0 3.2 %collective-permute-done.12.refs_10_ = bf16[2,16,4096]{2,1,0:T(8,128)(2,1)S(1)} collective-permute-done((bf16[2,16,4096]{2,1,0:T(8,128)(2,1)S(1)}, bf16[2,16,4096]{2,1,0:T(8,128)(2,1)S(1)}, u32[]{:S(2)}, u32[]{:S(2)}) %collective-permute-start.12) | collective-permute-done | bytes 262176 | tf_op jit(solution)/shard_map/ppermute | solution.py:307
  41.2 4.4 %shard_map.32 = (f32[64,4096]{1,0:T(8,128)S(1)}, bf16[64,4096]{1,0:T(8,128)(2,1)S(1)}) custom-call(bf16[2,16,4096]{2,1,0:T(8,128)(2,1)S(1)} %get-tuple-element.13.refs_0_, bf16[2,16,4096]{2,1,0:T(8,128)(2,1)S(1)} %collective-permute-done.refs_1_, bf16[2,16,4096]{2,1,0:T(8,128)(2,1)S(1)} %collective-permute-done.1.refs_2_, ...), custom_call_target="tpu_custom_call" | custom-call | flops 3221225472 | bytes 8388608 | tf_op jit(solution)/shard_map/pallas_call | solution.py:220
  45.6 0.1 collective-permute-start.17
  45.7 1.9 %collective-permute-done.17.part_ref = bf16[64,4096]{1,0:T(8,128)(2,1)S(1)} collective-permute-done((bf16[64,4096]{1,0:T(8,128)(2,1)S(1)}, bf16[64,4096]{1,0:T(8,128)(2,1)S(1)}, u32[]{:S(2)}, u32[]{:S(2)}) %collective-permute-start.17) | collective-permute-done | bytes 524320 | tf_op jit(solution)/shard_map/ppermute | solution.py:307
  47.6 0.1 shard_map.33
  47.7 21.0 %all_to_all.10.x_ref = bf16[32,16,512]{2,1,0:T(8,128)(2,1)S(1)} all-to-all(bf16[32,16,512]{2,1,0:T(8,128)(2,1)S(1)} %bitcast.1), channel_id=1, replica_groups=mesh['blk'=8,'grid'=4] {'blk','grid'}, dimensions={0} | all-to-all | bytes 1048576 | tf_op jit(solution)/shard_map/all_to_all | solution.py:367
  68.7 0.7 shard_map.34
  69.4 11.0 %all_to_all.11.parts_ref = f32[32,8,128]{2,1,0:T(8,128)S(1)} all-to-all(f32[32,8,128]{2,1,0:T(8,128)S(1)} %shard_map.34), channel_id=1, replica_groups=mesh['blk'=8,'grid'=4] {'blk','grid'}, dimensions={0} | all-to-all | bytes 262144 | tf_op jit(solution)/shard_map/all_to_all | solution.py:379
  80.4 2.4 %shard_map.35 = (bf16[32,16,512]{2,1,0:T(8,128)(2,1)}, f32[32,32]{1,0:T(8,128)}) custom-call(f32[32,8,128]{2,1,0:T(8,128)S(1)} %all_to_all.11.parts_ref, bf16[32,16,512]{2,1,0:T(8,128)(2,1)S(1)} %all_to_all.10.x_ref), custom_call_target="tpu_custom_call" | custom-call | tf_op jit(solution)/shard_map/pallas_call | solution.py:380
  (6 shorter events, 0.2 us)
Async XLA Ops:
  1.7 6.8 %collective-permute-start = (bf16[2,16,4096]{2,1,0:T(8,128)(2,1)S(1)}, bf16[2,16,4096]{2,1,0:T(8,128)(2,1)S(1)}, u32[]{:S(2)}, u32[]{:S(2)}) collective-permute-start(bf16[2,16,4096]{2,1,0:T(8,128)(2,1)S(1)} %get-tuple-element.14.refs_4_), channel_id=1, source_target_pairs={{0,1},{1,0},{2,3},{3,2},{4,5},{5,4},{6,7},{7,6},{8,9},{9,8},{10,11... | collective-permute-start | bytes 786440 | tf_op jit(solution)/shard_map/ppermute | solution.py:307
  2.3 14.5 %collective-permute-start.5 = (bf16[2,16,4096]{2,1,0:T(8,128)(2,1)S(1)}, bf16[2,16,4096]{2,1,0:T(8,128)(2,1)S(1)}, u32[]{:S(2)}, u32[]{:S(2)}) collective-permute-start(bf16[2,16,4096]{2,1,0:T(8,128)(2,1)S(1)} %get-tuple-element.13.refs_0_), channel_id=1, source_target_pairs={{0,8},{4,12},{8,16},{12,20},{16,24},{20,28},{24,0},{28,4},{1,9},{5... | collective-permute-start | bytes 786440 | tf_op jit(solution)/shard_map/ppermute | solution.py:323
  4.9 20.4 %collective-permute-start.3 = (bf16[2,16,4096]{2,1,0:T(8,128)(2,1)S(1)}, bf16[2,16,4096]{2,1,0:T(8,128)(2,1)S(1)}, u32[]{:S(2)}, u32[]{:S(2)}) collective-permute-start(bf16[2,16,4096]{2,1,0:T(8,128)(2,1)S(1)} %get-tuple-element.13.refs_0_), channel_id=1, source_target_pairs={{0,1},{3,2},{4,5},{7,6},{8,9},{11,10},{12,13},{15,14},{16,17},{19,... | collective-permute-start | bytes 786440 | tf_op jit(solution)/shard_map/ppermute | solution.py:307
  7.0 8.4 %collective-permute-start.1 = (bf16[2,16,4096]{2,1,0:T(8,128)(2,1)S(1)}, bf16[2,16,4096]{2,1,0:T(8,128)(2,1)S(1)}, u32[]{:S(2)}, u32[]{:S(2)}) collective-permute-start(bf16[2,16,4096]{2,1,0:T(8,128)(2,1)S(1)} %get-tuple-element.13.refs_0_), channel_id=1, source_target_pairs={{0,2},{1,3},{2,0},{3,1},{4,6},{5,7},{6,4},{7,5},{8,10},{9,11},{10,... | collective-permute-start | bytes 786440 | tf_op jit(solution)/shard_map/ppermute | solution.py:307
  8.6 9.8 %collective-permute-start.7 = (bf16[1,16,4096]{2,1,0:T(8,128)(2,1)S(1)}, bf16[1,16,4096]{2,1,0:T(8,128)(2,1)S(1)}, u32[]{:S(2)}, u32[]{:S(2)}) collective-permute-start(bf16[1,16,4096]{2,1,0:T(8,128)(2,1)S(1)} %get-tuple-element.15), channel_id=1, source_target_pairs={{0,8},{4,12},{8,16},{12,20},{16,24},{20,28},{24,0},{28,4},{1,9},{5... | collective-permute-start | bytes 393224 | tf_op jit(solution)/shard_map/ppermute | solution.py:323
  10.2 9.8 %collective-permute-start.9 = (bf16[1,16,4096]{2,1,0:T(8,128)(2,1)S(1)}, bf16[1,16,4096]{2,1,0:T(8,128)(2,1)S(1)}, u32[]{:S(2)}, u32[]{:S(2)}) collective-permute-start(bf16[1,16,4096]{2,1,0:T(8,128)(2,1)S(1)} %get-tuple-element.16), channel_id=1, source_target_pairs={{0,8},{4,12},{8,16},{12,20},{16,24},{20,28},{24,0},{28,4},{1,9},{5... | collective-permute-start | bytes 393224 | tf_op jit(solution)/shard_map/ppermute | solution.py:323
  15.4 8.2 %collective-permute-start.2 = (bf16[2,16,4096]{2,1,0:T(8,128)(2,1)S(1)}, bf16[2,16,4096]{2,1,0:T(8,128)(2,1)S(1)}, u32[]{:S(2)}, u32[]{:S(2)}) collective-permute-start(bf16[2,16,4096]{2,1,0:T(8,128)(2,1)S(1)} %collective-permute-done.refs_1_), channel_id=1, source_target_pairs={{0,2},{1,3},{2,0},{3,1},{4,6},{5,7},{6,4},{7,5},{8,10},{9,11},{10,... | collective-permute-start | bytes 786440 | tf_op jit(solution)/shard_map/ppermute | solution.py:307
  16.8 10.0 %collective-permute-start.11 = (bf16[2,16,4096]{2,1,0:T(8,128)(2,1)S(1)}, bf16[2,16,4096]{2,1,0:T(8,128)(2,1)S(1)}, u32[]{:S(2)}, u32[]{:S(2)}) collective-permute-start(bf16[2,16,4096]{2,1,0:T(8,128)(2,1)S(1)} %collective-permute-done.1.refs_2_), channel_id=1, source_target_pairs={{0,8},{4,12},{8,16},{12,20},{16,24},{20,28},{24,0},{28,4},{1,9},{5... | collective-permute-start | bytes 786440 | tf_op jit(solution)/shard_map/ppermute | solution.py:323
  18.4 9.7 %collective-permute-start.8 = (bf16[1,16,4096]{2,1,0:T(8,128)(2,1)S(1)}, bf16[1,16,4096]{2,1,0:T(8,128)(2,1)S(1)}, u32[]{:S(2)}, u32[]{:S(2)}) collective-permute-start(bf16[1,16,4096]{2,1,0:T(8,128)(2,1)S(1)} %broadcast_select_fusion.3), channel_id=1, source_target_pairs={{0,4},{4,0},{8,12},{12,8},{16,20},{20,16},{24,28},{28,24},{1,5},{5... | collective-permute-start | bytes 393224 | tf_op jit(solution)/shard_map/ppermute | solution.py:307
  20.0 11.3 %collective-permute-start.10 = (bf16[1,16,4096]{2,1,0:T(8,128)(2,1)S(1)}, bf16[1,16,4096]{2,1,0:T(8,128)(2,1)S(1)}, u32[]{:S(2)}, u32[]{:S(2)}) collective-permute-start(bf16[1,16,4096]{2,1,0:T(8,128)(2,1)S(1)} %broadcast_select_fusion.2), channel_id=1, source_target_pairs={{0,4},{4,0},{8,12},{12,8},{16,20},{20,16},{24,28},{28,24},{1,5},{5... | collective-permute-start | bytes 393224 | tf_op jit(solution)/shard_map/ppermute | solution.py:307
  23.5 6.3 %collective-permute-start.15 = (bf16[1,16,4096]{2,1,0:T(8,128)(2,1)S(1)}, bf16[1,16,4096]{2,1,0:T(8,128)(2,1)S(1)}, u32[]{:S(2)}, u32[]{:S(2)}) collective-permute-start(bf16[1,16,4096]{2,1,0:T(8,128)(2,1)S(1)} %collective-permute-done.7.refs_8_), channel_id=1, source_target_pairs={{0,2},{1,3},{2,0},{3,1},{4,6},{5,7},{6,4},{7,5},{8,10},{9,11},{10,... | collective-permute-start | bytes 393224 | tf_op jit(solution)/shard_map/ppermute | solution.py:307
  25.3 7.7 %collective-permute-start.16 = (bf16[1,16,4096]{2,1,0:T(8,128)(2,1)S(1)}, bf16[1,16,4096]{2,1,0:T(8,128)(2,1)S(1)}, u32[]{:S(2)}, u32[]{:S(2)}) collective-permute-start(bf16[1,16,4096]{2,1,0:T(8,128)(2,1)S(1)} %collective-permute-done.9.refs_9_), channel_id=1, source_target_pairs={{0,2},{1,3},{2,0},{3,1},{4,6},{5,7},{6,4},{7,5},{8,10},{9,11},{10,... | collective-permute-start | bytes 393224 | tf_op jit(solution)/shard_map/ppermute | solution.py:307
  26.8 6.6 %collective-permute-start.4 = (bf16[4,16,4096]{2,1,0:T(8,128)(2,1)S(1)}, bf16[4,16,4096]{2,1,0:T(8,128)(2,1)S(1)}, u32[]{:S(2)}, u32[]{:S(2)}) collective-permute-start(bf16[4,16,4096]{2,1,0:T(8,128)(2,1)S(1)} %pad_maximum_fusion), channel_id=1, source_target_pairs={{0,1},{3,2},{4,5},{7,6},{8,9},{11,10},{12,13},{15,14},{16,17},{19,... | collective-permute-start | bytes 1572872 | tf_op jit(solution)/shard_map/ppermute | solution.py:307
  28.1 9.6 %collective-permute-start.6 = (bf16[2,16,4096]{2,1,0:T(8,128)(2,1)S(1)}, bf16[2,16,4096]{2,1,0:T(8,128)(2,1)S(1)}, u32[]{:S(2)}, u32[]{:S(2)}) collective-permute-start(bf16[2,16,4096]{2,1,0:T(8,128)(2,1)S(1)} %broadcast_select_fusion.1), channel_id=1, source_target_pairs={{0,4},{4,0},{8,12},{12,8},{16,20},{20,16},{24,28},{28,24},{1,5},{5... | collective-permute-start | bytes 786440 | tf_op jit(solution)/shard_map/ppermute | solution.py:307
  29.8 11.3 %collective-permute-start.12 = (bf16[2,16,4096]{2,1,0:T(8,128)(2,1)S(1)}, bf16[2,16,4096]{2,1,0:T(8,128)(2,1)S(1)}, u32[]{:S(2)}, u32[]{:S(2)}) collective-permute-start(bf16[2,16,4096]{2,1,0:T(8,128)(2,1)S(1)} %broadcast_select_fusion), channel_id=1, source_target_pairs={{0,4},{4,0},{8,12},{12,8},{16,20},{20,16},{24,28},{28,24},{1,5},{5... | collective-permute-start | bytes 786440 | tf_op jit(solution)/shard_map/ppermute | solution.py:307
  31.4 6.4 %collective-permute-start.13 = (bf16[1,16,4096]{2,1,0:T(8,128)(2,1)S(1)}, bf16[1,16,4096]{2,1,0:T(8,128)(2,1)S(1)}, u32[]{:S(2)}, u32[]{:S(2)}) collective-permute-start(bf16[1,16,4096]{2,1,0:T(8,128)(2,1)S(1)} %collective-permute-done.8.refs_8_), channel_id=1, source_target_pairs={{0,2},{1,3},{2,0},{3,1},{4,6},{5,7},{6,4},{7,5},{8,10},{9,11},{10,... | collective-permute-start | bytes 393224 | tf_op jit(solution)/shard_map/ppermute | solution.py:307
  33.0 5.0 %collective-permute-start.14 = (bf16[1,16,4096]{2,1,0:T(8,128)(2,1)S(1)}, bf16[1,16,4096]{2,1,0:T(8,128)(2,1)S(1)}, u32[]{:S(2)}, u32[]{:S(2)}) collective-permute-start(bf16[1,16,4096]{2,1,0:T(8,128)(2,1)S(1)} %collective-permute-done.10.refs_9_), channel_id=1, source_target_pairs={{0,2},{1,3},{2,0},{3,1},{4,6},{5,7},{6,4},{7,5},{8,10},{9,11},{10,... | collective-permute-start | bytes 393224 | tf_op jit(solution)/shard_map/ppermute | solution.py:307
  45.6 2.0 %collective-permute-start.17 = (bf16[64,4096]{1,0:T(8,128)(2,1)S(1)}, bf16[64,4096]{1,0:T(8,128)(2,1)S(1)}, u32[]{:S(2)}, u32[]{:S(2)}) collective-permute-start(bf16[64,4096]{1,0:T(8,128)(2,1)S(1)} %get-tuple-element.23), channel_id=1, source_target_pairs={{0,1},{1,0},{2,3},{3,2},{4,5},{5,4},{6,7},{7,6},{8,9},{9,8},{10,11... | collective-permute-start | bytes 1572872 | tf_op jit(solution)/shard_map/ppermute | solution.py:307
where the time goes:
time: 83 us; the launch traced here: 82.8 us
  blocking collectives  32 us (39%)
  starting transfers between devices  23.5 us (28%)
  Pallas kernels  12.8 us (15%)
  waiting for transfers between devices  12.4 us (15%)
  local copies, waits for them, and re-layouts  1.09 us (1%)
    all_to_all x1, blocking collectives, body(): cellwise = lax.all_to_all(updated, ('blk', 'grid'), 0, 0, tiled=True)  21 us
    ppermute x14, starting transfers between devices, exchanged(): lax.ppermute(x, axis, [(i, i ^ by) for i in range(lax.axis_size(axis)) if...  16.1 us
    ppermute x14, waiting for transfers between devices, exchanged(): lax.ppermute(x, axis, [(i, i ^ by) for i in range(lax.axis_size(axis)) if...  11.3 us
    all_to_all x1, blocking collectives, body(): parts = lax.all_to_all(local, ('blk', 'grid'), 0, 0, tiled=True)  11 us
    pallas_call x2, Pallas kernels, add_block(): pl.pallas_call(lambda *refs: block_kernel(counts, final, refs), out_shape...  8.8 us
    ppermute x4, starting transfers between devices, shifted(): lax.ppermute(x, 'blk', [(i, (i + 2) % blocks) for i in range(blocks)])  7.41 us
    pallas_call x1, Pallas kernels, body(): pl.pallas_call(functools.partial(rotate_kernel, 1.0 / cell_count), out_sh...  2.37 us
  transfers between devices with their start and end apart: 18, of which 7 were waited for; matrix products, arithmetic and copies ran while one was open for 0% of the time, Pallas kernels for 6%

commit v1 on v0

--- a/solution.py
+++ b/solution.py
@@ -333,17 +333,13 @@
     give = lax.dynamic_slice_in_dim(orbitals, (1 - core) * half, half, 0)
     keep, give = lax.optimization_barrier((keep, give))
     held = [keep, exchanged(give, "grid", 1)]
-    pieces = [held[0]] + list(lax.optimization_barrier(
-        tuple(held[1][j:j + 1] for j in range(half))))
-    far = [shifted(piece) for piece in pieces]
+    far = [shifted(held[i]) for i in range(2)]
     across = [exchanged(held[i], "grid", top) for i in range(2)]
-    near = [relayed(piece, far[i]) for i, piece in enumerate(pieces)]
-    far_other = [shifted(across[0])] + [
-        exchanged(far[i], "grid", top) for i in range(1, len(far))]
-    relay, diagonals, weights = lax.optimization_barrier((across[0], diagonals, weights))
+    near = [relayed(held[i], far[i]) for i in range(2)]
+    far_other = [exchanged(far[0], "grid", top), shifted(across[1])]
+    relay, diagonals, weights = lax.optimization_barrier((across[1], diagonals, weights))
     tables = (diagonals, weights)
-    near_other = [relayed(relay, far_other[0])] + [
-        exchanged(near[i], "grid", top) for i in range(1, len(near))]
+    near_other = [exchanged(near[0], "grid", top), relayed(relay, far_other[1])]
     local = held + across
     passed = [give, passed_on(held[0]), passed_on(jnp.concatenate([across[1], across[0]], 0))]
     acc = add_block(local, passed, far + far_other, tables, None)

time: 83 us -> 79.1 us (0.953)
  starting transfers between devices: 23.5 us -> 18.7 us
  waiting for transfers between devices: 12.4 us -> 16.7 us
  blocking collectives: 32 us -> 28.7 us
    ppermute x4 -> x3, waiting for transfers between devices: 1.12 us -> 11.8 us  [shifted(): lax.ppermute(x, 'blk', [(i, (i + 2) % blocks) for i in range(blocks)])]
    ppermute x14 -> x11, waiting for transfers between devices: 11.3 us -> 4.93 us  [exchanged(): lax.ppermute(x, axis, [(i, i ^ by) for i in range(lax.axis_size(axis)) if...]
    all_to_all x1, blocking collectives: 21 us -> 17.7 us  [body(): cellwise = lax.all_to_all(updated, ('blk', 'grid'), 0, 0, tiled=True)]
    ppermute x14 -> x11, starting transfers between devices: 16.1 us -> 13.7 us  [exchanged(): lax.ppermute(x, axis, [(i, i ^ by) for i in range(lax.axis_size(axis)) if...]
    ppermute x4 -> x3, starting transfers between devices: 7.41 us -> 5.01 us  [shifted(): lax.ppermute(x, 'blk', [(i, (i + 2) % blocks) for i in range(blocks)])]
  transfers between devices with their start and end apart: 18 -> 14, of which waited for: 7 -> 5; matrix products, arithmetic and copies ran while one was open for 0% -> 0% of each run, Pallas kernels for 6% -> 7%
where the time goes in v1:
time: 79.1 us; the launch traced here: 78.9 us
  blocking collectives  28.7 us (36%)
  starting transfers between devices  18.7 us (24%)
  waiting for transfers between devices  16.7 us (21%)
  Pallas kernels  12.8 us (16%)
  local copies, waits for them, and re-layouts  1.07 us (1%)
    all_to_all x1, blocking collectives, body(): cellwise = lax.all_to_all(updated, ('blk', 'grid'), 0, 0, tiled=True)  17.7 us
    ppermute x11, starting transfers between devices, exchanged(): lax.ppermute(x, axis, [(i, i ^ by) for i in range(lax.axis_size(axis)) if...  13.7 us
    ppermute x3, waiting for transfers between devices, shifted(): lax.ppermute(x, 'blk', [(i, (i + 2) % blocks) for i in range(blocks)])  11.8 us
    all_to_all x1, blocking collectives, body(): parts = lax.all_to_all(local, ('blk', 'grid'), 0, 0, tiled=True)  11 us
    pallas_call x2, Pallas kernels, add_block(): pl.pallas_call(lambda *refs: block_kernel(counts, final, refs), out_shape...  8.8 us
    ppermute x3, starting transfers between devices, shifted(): lax.ppermute(x, 'blk', [(i, (i + 2) % blocks) for i in range(blocks)])  5.01 us
    ppermute x11, waiting for transfers between devices, exchanged(): lax.ppermute(x, axis, [(i, i ^ by) for i in range(lax.axis_size(axis)) if...  4.93 us
    pallas_call x1, Pallas kernels, body(): pl.pallas_call(functools.partial(rotate_kernel, 1.0 / cell_count), out_sh...  2.37 us
  transfers between devices with their start and end apart: 14, of which 5 were waited for; matrix products, arithmetic and copies ran while one was open for 0% of the time, Pallas kernels for 7%

profile of v1, /device:TPU:0, one launch (start us, length us, event | category | flops | bytes accessed | tf_op | source)
XLA Modules:
  0.0 78.9 jit_solution(12309193415475046158)
XLA Ops:
  0.6 1.1 %constant_dynamic-slice_fusion = (bf16[2,16,4096]{2,1,0:T(8,128)(2,1)S(1)}, bf16[2,16,4096]{2,1,0:T(8,128)(2,1)S(1)}) fusion(bf16[4,16,4096]{2,1,0:T(8,128)(2,1)} %param.1, s32[]{:T(128)S(6)} %select_n.35, s32[]{:T(128)S(6)} %select_n.34), kind=kLoop, calls=%fused_computation.4 | loop fusion | bytes 1048584 | tf_op jit(solution)/shard_map/dynamic_slice | solution.py:333
  1.7 0.6 collective-permute-start
  2.3 2.6 %collective-permute-start.5 = (bf16[2,16,4096]{2,1,0:T(8,128)(2,1)S(1)}, bf16[2,16,4096]{2,1,0:T(8,128)(2,1)S(1)}, u32[]{:S(2)}, u32[]{:S(2)}) collective-permute-start(bf16[2,16,4096]{2,1,0:T(8,128)(2,1)S(1)} %get-tuple-element.11.refs_0_), channel_id=1, source_target_pairs={{0,8},{4,12},{8,16},{12,20},{16,24},{20,28},{24,0},{28,4},{1,9},{5... | collective-permute-start | bytes 786440 | tf_op jit(solution)/shard_map/ppermute | solution.py:323
  4.9 2.1 %collective-permute-start.3 = (bf16[2,16,4096]{2,1,0:T(8,128)(2,1)S(1)}, bf16[2,16,4096]{2,1,0:T(8,128)(2,1)S(1)}, u32[]{:S(2)}, u32[]{:S(2)}) collective-permute-start(bf16[2,16,4096]{2,1,0:T(8,128)(2,1)S(1)} %get-tuple-element.11.refs_0_), channel_id=1, source_target_pairs={{0,1},{3,2},{4,5},{7,6},{8,9},{11,10},{12,13},{15,14},{16,17},{19,... | collective-permute-start | bytes 786440 | tf_op jit(solution)/shard_map/ppermute | solution.py:307
  7.0 0.8 collective-permute-start.1
  7.8 0.8 %shard_map.30 = (bf16[4,256,256]{2,1,0:T(8,128)(2,1)S(1)}, f32[4096,128]{1,0:T(8,128)S(1)}) custom-call(), custom_call_target="tpu_custom_call" | custom-call | flops 268435456 | bytes 3145728 | tf_op jit(solution)/shard_map/pallas_call | solution.py:83
  8.6 0.0 collective-permute-done.refs_1_
  8.6 1.6 %collective-permute-start.7 = (bf16[2,16,4096]{2,1,0:T(8,128)(2,1)S(1)}, bf16[2,16,4096]{2,1,0:T(8,128)(2,1)S(1)}, u32[]{:S(2)}, u32[]{:S(2)}) collective-permute-start(bf16[2,16,4096]{2,1,0:T(8,128)(2,1)S(1)} %collective-permute-done.refs_1_), channel_id=1, source_target_pairs={{0,8},{4,12},{8,16},{12,20},{16,24},{20,28},{24,0},{28,4},{1,9},{5... | collective-permute-start | bytes 786440 | tf_op jit(solution)/shard_map/ppermute | solution.py:323
  10.2 3.6 %collective-permute-done.5.refs_7_ = bf16[2,16,4096]{2,1,0:T(8,128)(2,1)S(1)} collective-permute-done((bf16[2,16,4096]{2,1,0:T(8,128)(2,1)S(1)}, bf16[2,16,4096]{2,1,0:T(8,128)(2,1)S(1)}, u32[]{:S(2)}, u32[]{:S(2)}) %collective-permute-start.5) | collective-permute-done | bytes 262176 | tf_op jit(solution)/shard_map/ppermute | solution.py:323
  13.9 1.6 %collective-permute-start.6 = (bf16[2,16,4096]{2,1,0:T(8,128)(2,1)S(1)}, bf16[2,16,4096]{2,1,0:T(8,128)(2,1)S(1)}, u32[]{:S(2)}, u32[]{:S(2)}) collective-permute-start(bf16[2,16,4096]{2,1,0:T(8,128)(2,1)S(1)} %broadcast_select_fusion.2), channel_id=1, source_target_pairs={{0,4},{4,0},{8,12},{12,8},{16,20},{20,16},{24,28},{28,24},{1,5},{5... | collective-permute-start | bytes 786440 | tf_op jit(solution)/shard_map/ppermute | solution.py:307
  15.5 2.0 %collective-permute-start.2 = (bf16[2,16,4096]{2,1,0:T(8,128)(2,1)S(1)}, bf16[2,16,4096]{2,1,0:T(8,128)(2,1)S(1)}, u32[]{:S(2)}, u32[]{:S(2)}) collective-permute-start(bf16[2,16,4096]{2,1,0:T(8,128)(2,1)S(1)} %collective-permute-done.refs_1_), channel_id=1, source_target_pairs={{0,2},{1,3},{2,0},{3,1},{4,6},{5,7},{6,4},{7,5},{8,10},{9,11},{10,... | collective-permute-start | bytes 786440 | tf_op jit(solution)/shard_map/ppermute | solution.py:307
  17.4 2.1 %collective-permute-done.7.refs_8_ = bf16[2,16,4096]{2,1,0:T(8,128)(2,1)S(1)} collective-permute-done((bf16[2,16,4096]{2,1,0:T(8,128)(2,1)S(1)}, bf16[2,16,4096]{2,1,0:T(8,128)(2,1)S(1)}, u32[]{:S(2)}, u32[]{:S(2)}) %collective-permute-start.7) | collective-permute-done | bytes 262176 | tf_op jit(solution)/shard_map/ppermute | solution.py:323
  19.5 1.5 %collective-permute-start.12 = (bf16[2,16,4096]{2,1,0:T(8,128)(2,1)S(1)}, bf16[2,16,4096]{2,1,0:T(8,128)(2,1)S(1)}, u32[]{:S(2)}, u32[]{:S(2)}) collective-permute-start(bf16[2,16,4096]{2,1,0:T(8,128)(2,1)S(1)} %collective-permute-done.5.refs_7_), channel_id=1, source_target_pairs={{0,2},{1,3},{2,0},{3,1},{4,6},{5,7},{6,4},{7,5},{8,10},{9,11},{10,... | collective-permute-start | bytes 786440 | tf_op jit(solution)/shard_map/ppermute | solution.py:307
  21.0 3.0 %collective-permute-done.2.refs_3_ = bf16[2,16,4096]{2,1,0:T(8,128)(2,1)S(1)} collective-permute-done((bf16[2,16,4096]{2,1,0:T(8,128)(2,1)S(1)}, bf16[2,16,4096]{2,1,0:T(8,128)(2,1)S(1)}, u32[]{:S(2)}, u32[]{:S(2)}) %collective-permute-start.2) | collective-permute-done | bytes 262176 | tf_op jit(solution)/shard_map/ppermute | solution.py:307
  24.0 0.0 collective-permute-start.8
  24.0 0.0 collective-permute-done.1.refs_2_
  24.0 0.8 collective-permute-start.10
  24.8 0.0 collective-permute-done.6.refs_7_
  24.8 1.3 %collective-permute-start.4 = (bf16[4,16,4096]{2,1,0:T(8,128)(2,1)S(1)}, bf16[4,16,4096]{2,1,0:T(8,128)(2,1)S(1)}, u32[]{:S(2)}, u32[]{:S(2)}) collective-permute-start(bf16[4,16,4096]{2,1,0:T(8,128)(2,1)S(1)} %pad_maximum_fusion), channel_id=1, source_target_pairs={{0,1},{3,2},{4,5},{7,6},{8,9},{11,10},{12,13},{15,14},{16,17},{19,... | collective-permute-start | bytes 1572872 | tf_op jit(solution)/shard_map/ppermute | solution.py:307
  26.2 6.1 %collective-permute-done.10.refs_10_ = bf16[2,16,4096]{2,1,0:T(8,128)(2,1)S(1)} collective-permute-done((bf16[2,16,4096]{2,1,0:T(8,128)(2,1)S(1)}, bf16[2,16,4096]{2,1,0:T(8,128)(2,1)S(1)}, u32[]{:S(2)}, u32[]{:S(2)}) %collective-permute-start.10) | collective-permute-done | bytes 262176 | tf_op jit(solution)/shard_map/ppermute | solution.py:323
  32.2 1.8 %collective-permute-start.9 = (bf16[2,16,4096]{2,1,0:T(8,128)(2,1)S(1)}, bf16[2,16,4096]{2,1,0:T(8,128)(2,1)S(1)}, u32[]{:S(2)}, u32[]{:S(2)}) collective-permute-start(bf16[2,16,4096]{2,1,0:T(8,128)(2,1)S(1)} %collective-permute-done.6.refs_7_), channel_id=1, source_target_pairs={{0,2},{1,3},{2,0},{3,1},{4,6},{5,7},{6,4},{7,5},{8,10},{9,11},{10,... | collective-permute-start | bytes 786440 | tf_op jit(solution)/shard_map/ppermute | solution.py:307
  34.1 0.0 collective-permute-done.3.refs_5_
  34.1 2.1 %collective-permute-start.11 = (bf16[2,16,4096]{2,1,0:T(8,128)(2,1)S(1)}, bf16[2,16,4096]{2,1,0:T(8,128)(2,1)S(1)}, u32[]{:S(2)}, u32[]{:S(2)}) collective-permute-start(bf16[2,16,4096]{2,1,0:T(8,128)(2,1)S(1)} %broadcast_select_fusion), channel_id=1, source_target_pairs={{0,4},{4,0},{8,12},{12,8},{16,20},{20,16},{24,28},{28,24},{1,5},{5... | collective-permute-start | bytes 786440 | tf_op jit(solution)/shard_map/ppermute | solution.py:307
  36.2 0.0 collective-permute-done.12.refs_9_
  36.2 0.0 collective-permute-done.4.refs_6_
  36.2 4.4 %shard_map.31.refs_13_ = f32[2,64,4096]{2,1,0:T(8,128)S(1)} custom-call(bf16[2,16,4096]{2,1,0:T(8,128)(2,1)S(1)} %get-tuple-element.11.refs_0_, bf16[2,16,4096]{2,1,0:T(8,128)(2,1)S(1)} %collective-permute-done.refs_1_, bf16[2,16,4096]{2,1,0:T(8,128)(2,1)S(1)} %collective-permute-done.1.refs_2_, bf16[2,16,4096]{2,1,0:T(8,128)(2,1)S(1)} %collective-permute-done.2.refs_3_, ...), custom_call_target="tpu_custom_call" | custom-call | flops 3221225472 | bytes 8388608 | tf_op jit(solution)/shard_map/pallas_call | solution.py:220
  40.6 0.0 collective-permute-done.8.refs_8_
  40.6 0.0 collective-permute-done.9.refs_9_
  40.6 0.0 collective-permute-done.11.refs_10_
  40.6 4.4 %shard_map.32 = (f32[64,4096]{1,0:T(8,128)S(1)}, bf16[64,4096]{1,0:T(8,128)(2,1)S(1)}) custom-call(bf16[2,16,4096]{2,1,0:T(8,128)(2,1)S(1)} %get-tuple-element.11.refs_0_, bf16[2,16,4096]{2,1,0:T(8,128)(2,1)S(1)} %collective-permute-done.refs_1_, bf16[2,16,4096]{2,1,0:T(8,128)(2,1)S(1)} %collective-permute-done.1.refs_2_, ...), custom_call_target="tpu_custom_call" | custom-call | flops 3221225472 | bytes 8388608 | tf_op jit(solution)/shard_map/pallas_call | solution.py:220
  45.0 0.1 collective-permute-start.13
  45.1 1.9 %collective-permute-done.13.part_ref = bf16[64,4096]{1,0:T(8,128)(2,1)S(1)} collective-permute-done((bf16[64,4096]{1,0:T(8,128)(2,1)S(1)}, bf16[64,4096]{1,0:T(8,128)(2,1)S(1)}, u32[]{:S(2)}, u32[]{:S(2)}) %collective-permute-start.13) | collective-permute-done | bytes 524320 | tf_op jit(solution)/shard_map/ppermute | solution.py:307
  47.0 0.1 shard_map.33
  47.1 17.7 %all_to_all.10.x_ref = bf16[32,16,512]{2,1,0:T(8,128)(2,1)S(1)} all-to-all(bf16[32,16,512]{2,1,0:T(8,128)(2,1)S(1)} %bitcast.1), channel_id=1, replica_groups=mesh['blk'=8,'grid'=4] {'blk','grid'}, dimensions={0} | all-to-all | bytes 1048576 | tf_op jit(solution)/shard_map/all_to_all | solution.py:363
  64.8 0.7 shard_map.34
  65.5 11.0 %all_to_all.11.parts_ref = f32[32,8,128]{2,1,0:T(8,128)S(1)} all-to-all(f32[32,8,128]{2,1,0:T(8,128)S(1)} %shard_map.34), channel_id=1, replica_groups=mesh['blk'=8,'grid'=4] {'blk','grid'}, dimensions={0} | all-to-all | bytes 262144 | tf_op jit(solution)/shard_map/all_to_all | solution.py:375
  76.5 2.4 %shard_map.35 = (bf16[32,16,512]{2,1,0:T(8,128)(2,1)}, f32[32,32]{1,0:T(8,128)}) custom-call(f32[32,8,128]{2,1,0:T(8,128)S(1)} %all_to_all.11.parts_ref, bf16[32,16,512]{2,1,0:T(8,128)(2,1)S(1)} %all_to_all.10.x_ref), custom_call_target="tpu_custom_call" | custom-call | tf_op jit(solution)/shard_map/pallas_call | solution.py:376
  (4 shorter events, 0.1 us)
Async XLA Ops:
  1.7 6.8 %collective-permute-start = (bf16[2,16,4096]{2,1,0:T(8,128)(2,1)S(1)}, bf16[2,16,4096]{2,1,0:T(8,128)(2,1)S(1)}, u32[]{:S(2)}, u32[]{:S(2)}) collective-permute-start(bf16[2,16,4096]{2,1,0:T(8,128)(2,1)S(1)} %get-tuple-element.12.refs_4_), channel_id=1, source_target_pairs={{0,1},{1,0},{2,3},{3,2},{4,5},{5,4},{6,7},{7,6},{8,9},{9,8},{10,11... | collective-permute-start | bytes 786440 | tf_op jit(solution)/shard_map/ppermute | solution.py:307
  2.3 11.6 %collective-permute-start.5 = (bf16[2,16,4096]{2,1,0:T(8,128)(2,1)S(1)}, bf16[2,16,4096]{2,1,0:T(8,128)(2,1)S(1)}, u32[]{:S(2)}, u32[]{:S(2)}) collective-permute-start(bf16[2,16,4096]{2,1,0:T(8,128)(2,1)S(1)} %get-tuple-element.11.refs_0_), channel_id=1, source_target_pairs={{0,8},{4,12},{8,16},{12,20},{16,24},{20,28},{24,0},{28,4},{1,9},{5... | collective-permute-start | bytes 786440 | tf_op jit(solution)/shard_map/ppermute | solution.py:323
  4.9 29.2 %collective-permute-start.3 = (bf16[2,16,4096]{2,1,0:T(8,128)(2,1)S(1)}, bf16[2,16,4096]{2,1,0:T(8,128)(2,1)S(1)}, u32[]{:S(2)}, u32[]{:S(2)}) collective-permute-start(bf16[2,16,4096]{2,1,0:T(8,128)(2,1)S(1)} %get-tuple-element.11.refs_0_), channel_id=1, source_target_pairs={{0,1},{3,2},{4,5},{7,6},{8,9},{11,10},{12,13},{15,14},{16,17},{19,... | collective-permute-start | bytes 786440 | tf_op jit(solution)/shard_map/ppermute | solution.py:307
  7.0 17.0 %collective-permute-start.1 = (bf16[2,16,4096]{2,1,0:T(8,128)(2,1)S(1)}, bf16[2,16,4096]{2,1,0:T(8,128)(2,1)S(1)}, u32[]{:S(2)}, u32[]{:S(2)}) collective-permute-start(bf16[2,16,4096]{2,1,0:T(8,128)(2,1)S(1)} %get-tuple-element.11.refs_0_), channel_id=1, source_target_pairs={{0,2},{1,3},{2,0},{3,1},{4,6},{5,7},{6,4},{7,5},{8,10},{9,11},{10,... | collective-permute-start | bytes 786440 | tf_op jit(solution)/shard_map/ppermute | solution.py:307
  8.6 10.9 %collective-permute-start.7 = (bf16[2,16,4096]{2,1,0:T(8,128)(2,1)S(1)}, bf16[2,16,4096]{2,1,0:T(8,128)(2,1)S(1)}, u32[]{:S(2)}, u32[]{:S(2)}) collective-permute-start(bf16[2,16,4096]{2,1,0:T(8,128)(2,1)S(1)} %collective-permute-done.refs_1_), channel_id=1, source_target_pairs={{0,8},{4,12},{8,16},{12,20},{16,24},{20,28},{24,0},{28,4},{1,9},{5... | collective-permute-start | bytes 786440 | tf_op jit(solution)/shard_map/ppermute | solution.py:323
  13.9 10.9 %collective-permute-start.6 = (bf16[2,16,4096]{2,1,0:T(8,128)(2,1)S(1)}, bf16[2,16,4096]{2,1,0:T(8,128)(2,1)S(1)}, u32[]{:S(2)}, u32[]{:S(2)}) collective-permute-start(bf16[2,16,4096]{2,1,0:T(8,128)(2,1)S(1)} %broadcast_select_fusion.2), channel_id=1, source_target_pairs={{0,4},{4,0},{8,12},{12,8},{16,20},{20,16},{24,28},{28,24},{1,5},{5... | collective-permute-start | bytes 786440 | tf_op jit(solution)/shard_map/ppermute | solution.py:307
  15.5 8.5 %collective-permute-start.2 = (bf16[2,16,4096]{2,1,0:T(8,128)(2,1)S(1)}, bf16[2,16,4096]{2,1,0:T(8,128)(2,1)S(1)}, u32[]{:S(2)}, u32[]{:S(2)}) collective-permute-start(bf16[2,16,4096]{2,1,0:T(8,128)(2,1)S(1)} %collective-permute-done.refs_1_), channel_id=1, source_target_pairs={{0,2},{1,3},{2,0},{3,1},{4,6},{5,7},{6,4},{7,5},{8,10},{9,11},{10,... | collective-permute-start | bytes 786440 | tf_op jit(solution)/shard_map/ppermute | solution.py:307
  19.5 16.7 %collective-permute-start.12 = (bf16[2,16,4096]{2,1,0:T(8,128)(2,1)S(1)}, bf16[2,16,4096]{2,1,0:T(8,128)(2,1)S(1)}, u32[]{:S(2)}, u32[]{:S(2)}) collective-permute-start(bf16[2,16,4096]{2,1,0:T(8,128)(2,1)S(1)} %collective-permute-done.5.refs_7_), channel_id=1, source_target_pairs={{0,2},{1,3},{2,0},{3,1},{4,6},{5,7},{6,4},{7,5},{8,10},{9,11},{10,... | collective-permute-start | bytes 786440 | tf_op jit(solution)/shard_map/ppermute | solution.py:307
  24.0 16.6 %collective-permute-start.8 = (bf16[2,16,4096]{2,1,0:T(8,128)(2,1)S(1)}, bf16[2,16,4096]{2,1,0:T(8,128)(2,1)S(1)}, u32[]{:S(2)}, u32[]{:S(2)}) collective-permute-start(bf16[2,16,4096]{2,1,0:T(8,128)(2,1)S(1)} %broadcast_select_fusion.1), channel_id=1, source_target_pairs={{0,4},{4,0},{8,12},{12,8},{16,20},{20,16},{24,28},{28,24},{1,5},{5... | collective-permute-start | bytes 786440 | tf_op jit(solution)/shard_map/ppermute | solution.py:307
  24.0 8.2 %collective-permute-start.10 = (bf16[2,16,4096]{2,1,0:T(8,128)(2,1)S(1)}, bf16[2,16,4096]{2,1,0:T(8,128)(2,1)S(1)}, u32[]{:S(2)}, u32[]{:S(2)}) collective-permute-start(bf16[2,16,4096]{2,1,0:T(8,128)(2,1)S(1)} %collective-permute-done.2.refs_3_), channel_id=1, source_target_pairs={{0,8},{4,12},{8,16},{12,20},{16,24},{20,28},{24,0},{28,4},{1,9},{5... | collective-permute-start | bytes 786440 | tf_op jit(solution)/shard_map/ppermute | solution.py:323
  24.8 11.4 %collective-permute-start.4 = (bf16[4,16,4096]{2,1,0:T(8,128)(2,1)S(1)}, bf16[4,16,4096]{2,1,0:T(8,128)(2,1)S(1)}, u32[]{:S(2)}, u32[]{:S(2)}) collective-permute-start(bf16[4,16,4096]{2,1,0:T(8,128)(2,1)S(1)} %pad_maximum_fusion), channel_id=1, source_target_pairs={{0,1},{3,2},{4,5},{7,6},{8,9},{11,10},{12,13},{15,14},{16,17},{19,... | collective-permute-start | bytes 1572872 | tf_op jit(solution)/shard_map/ppermute | solution.py:307
  32.2 8.4 %collective-permute-start.9 = (bf16[2,16,4096]{2,1,0:T(8,128)(2,1)S(1)}, bf16[2,16,4096]{2,1,0:T(8,128)(2,1)S(1)}, u32[]{:S(2)}, u32[]{:S(2)}) collective-permute-start(bf16[2,16,4096]{2,1,0:T(8,128)(2,1)S(1)} %collective-permute-done.6.refs_7_), channel_id=1, source_target_pairs={{0,2},{1,3},{2,0},{3,1},{4,6},{5,7},{6,4},{7,5},{8,10},{9,11},{10,... | collective-permute-start | bytes 786440 | tf_op jit(solution)/shard_map/ppermute | solution.py:307
  34.1 6.5 %collective-permute-start.11 = (bf16[2,16,4096]{2,1,0:T(8,128)(2,1)S(1)}, bf16[2,16,4096]{2,1,0:T(8,128)(2,1)S(1)}, u32[]{:S(2)}, u32[]{:S(2)}) collective-permute-start(bf16[2,16,4096]{2,1,0:T(8,128)(2,1)S(1)} %broadcast_select_fusion), channel_id=1, source_target_pairs={{0,4},{4,0},{8,12},{12,8},{16,20},{20,16},{24,28},{28,24},{1,5},{5... | collective-permute-start | bytes 786440 | tf_op jit(solution)/shard_map/ppermute | solution.py:307
  45.0 2.0 %collective-permute-start.13 = (bf16[64,4096]{1,0:T(8,128)(2,1)S(1)}, bf16[64,4096]{1,0:T(8,128)(2,1)S(1)}, u32[]{:S(2)}, u32[]{:S(2)}) collective-permute-start(bf16[64,4096]{1,0:T(8,128)(2,1)S(1)} %get-tuple-element.19), channel_id=1, source_target_pairs={{0,1},{1,0},{2,3},{3,2},{4,5},{5,4},{6,7},{7,6},{8,9},{9,8},{10,11... | collective-permute-start | bytes 1572872 | tf_op jit(solution)/shard_map/ppermute | solution.py:307

commit v2 on v1

--- a/solution.py
+++ b/solution.py
@@ -334,14 +334,17 @@
     keep, give = lax.optimization_barrier((keep, give))
     held = [keep, exchanged(give, "grid", 1)]
     far = [shifted(held[i]) for i in range(2)]
-    across = [exchanged(held[i], "grid", top) for i in range(2)]
+    across = [
+        exchanged(held[0], "grid", top, lambda i: i // 2 != i % 2), exchanged(held[1], "grid", top)
+    ]
     near = [relayed(held[i], far[i]) for i in range(2)]
     far_other = [exchanged(far[0], "grid", top), shifted(across[1])]
     relay, diagonals, weights = lax.optimization_barrier((across[1], diagonals, weights))
     tables = (diagonals, weights)
     near_other = [exchanged(near[0], "grid", top), relayed(relay, far_other[1])]
     local = held + across
-    passed = [give, passed_on(held[0]), passed_on(jnp.concatenate([across[1], across[0]], 0))]
+    joined = jnp.concatenate([across[1], across[0]], 0)
+    passed = [give, passed_on(held[0]), passed_on(joined)]
     acc = add_block(local, passed, far + far_other, tables, None)
     mine, other = add_block(local, passed, near + near_other, tables, acc)
     other = exchanged(other, "grid", 1)

time: 79.1 us -> 79.4 us (level)
  starting transfers between devices: 18.7 us -> 19.7 us
    ppermute x11, starting transfers between devices: 13.7 us -> 14.8 us  [exchanged(): lax.ppermute(x, axis, [(i, i ^ by) for i in range(lax.axis_size(axis)) if...]
where the time goes in v2:
time: 79.4 us; the launch traced here: 79.2 us
  blocking collectives  28.7 us (36%)
  starting transfers between devices  19.7 us (25%)
  waiting for transfers between devices  16 us (20%)
  Pallas kernels  12.8 us (16%)
  local copies, waits for them, and re-layouts  1.07 us (1%)
  between operations  0.8 us (1%)
    all_to_all x1, blocking collectives, body(): cellwise = lax.all_to_all(updated, ('blk', 'grid'), 0, 0, tiled=True)  17.7 us
    ppermute x11, starting transfers between devices, exchanged(): lax.ppermute(x, axis, [(i, i ^ by) for i in range(lax.axis_size(axis)) if...  14.8 us
    ppermute x3, waiting for transfers between devices, shifted(): lax.ppermute(x, 'blk', [(i, (i + 2) % blocks) for i in range(blocks)])  11.5 us
    all_to_all x1, blocking collectives, body(): parts = lax.all_to_all(local, ('blk', 'grid'), 0, 0, tiled=True)  11 us
    pallas_call x2, Pallas kernels, add_block(): pl.pallas_call(lambda *refs: block_kernel(counts, final, refs), out_shape...  8.8 us
    ppermute x3, starting transfers between devices, shifted(): lax.ppermute(x, 'blk', [(i, (i + 2) % blocks) for i in range(blocks)])  4.91 us
    ppermute x11, waiting for transfers between devices, exchanged(): lax.ppermute(x, axis, [(i, i ^ by) for i in range(lax.axis_size(axis)) if...  4.51 us
    pallas_call x1, Pallas kernels, body(): pl.pallas_call(functools.partial(rotate_kernel, 1.0 / cell_count), out_sh...  2.37 us
  transfers between devices with their start and end apart: 14, of which 5 were waited for; matrix products, arithmetic and copies ran while one was open for 0% of the time, Pallas kernels for 7%

profile of v2, /device:TPU:0, one launch (start us, length us, event | category | flops | bytes accessed | tf_op | source)
XLA Modules:
  0.0 79.2 jit_solution(11678728462858609171)
XLA Ops:
  0.6 1.1 %constant_dynamic-slice_fusion = (bf16[2,16,4096]{2,1,0:T(8,128)(2,1)S(1)}, bf16[2,16,4096]{2,1,0:T(8,128)(2,1)S(1)}) fusion(bf16[4,16,4096]{2,1,0:T(8,128)(2,1)} %param.1, s32[]{:T(128)S(6)} %select_n.35, s32[]{:T(128)S(6)} %select_n.34), kind=kLoop, calls=%fused_computation.4 | loop fusion | bytes 1048584 | tf_op jit(solution)/shard_map/dynamic_slice | solution.py:333
  1.7 0.6 collective-permute-start
  2.3 2.6 %collective-permute-start.5 = (bf16[2,16,4096]{2,1,0:T(8,128)(2,1)S(1)}, bf16[2,16,4096]{2,1,0:T(8,128)(2,1)S(1)}, u32[]{:S(2)}, u32[]{:S(2)}) collective-permute-start(bf16[2,16,4096]{2,1,0:T(8,128)(2,1)S(1)} %get-tuple-element.11.refs_0_), channel_id=1, source_target_pairs={{0,8},{4,12},{8,16},{12,20},{16,24},{20,28},{24,0},{28,4},{1,9},{5... | collective-permute-start | bytes 786440 | tf_op jit(solution)/shard_map/ppermute | solution.py:323
  4.9 2.1 %collective-permute-start.3 = (bf16[2,16,4096]{2,1,0:T(8,128)(2,1)S(1)}, bf16[2,16,4096]{2,1,0:T(8,128)(2,1)S(1)}, u32[]{:S(2)}, u32[]{:S(2)}) collective-permute-start(bf16[2,16,4096]{2,1,0:T(8,128)(2,1)S(1)} %get-tuple-element.11.refs_0_), channel_id=1, source_target_pairs={{0,1},{3,2},{4,5},{7,6},{8,9},{11,10},{12,13},{15,14},{16,17},{19,... | collective-permute-start | bytes 786440 | tf_op jit(solution)/shard_map/ppermute | solution.py:307
  7.0 1.3 %collective-permute-start.1 = (bf16[2,16,4096]{2,1,0:T(8,128)(2,1)S(1)}, bf16[2,16,4096]{2,1,0:T(8,128)(2,1)S(1)}, u32[]{:S(2)}, u32[]{:S(2)}) collective-permute-start(bf16[2,16,4096]{2,1,0:T(8,128)(2,1)S(1)} %get-tuple-element.11.refs_0_), channel_id=1, source_target_pairs={{1,3},{2,0},{5,7},{6,4},{9,11},{10,8},{13,15},{14,12},{17,19},{18,... | collective-permute-start | bytes 786440 | tf_op jit(solution)/shard_map/ppermute | solution.py:307
  8.3 0.8 %shard_map.30 = (bf16[4,256,256]{2,1,0:T(8,128)(2,1)S(1)}, f32[4096,128]{1,0:T(8,128)S(1)}) custom-call(), custom_call_target="tpu_custom_call" | custom-call | flops 268435456 | bytes 3145728 | tf_op jit(solution)/shard_map/pallas_call | solution.py:83
  9.1 0.0 collective-permute-done.refs_1_
  9.1 1.6 %collective-permute-start.7 = (bf16[2,16,4096]{2,1,0:T(8,128)(2,1)S(1)}, bf16[2,16,4096]{2,1,0:T(8,128)(2,1)S(1)}, u32[]{:S(2)}, u32[]{:S(2)}) collective-permute-start(bf16[2,16,4096]{2,1,0:T(8,128)(2,1)S(1)} %collective-permute-done.refs_1_), channel_id=1, source_target_pairs={{0,8},{4,12},{8,16},{12,20},{16,24},{20,28},{24,0},{28,4},{1,9},{5... | collective-permute-start | bytes 786440 | tf_op jit(solution)/shard_map/ppermute | solution.py:323
  10.8 3.1 %collective-permute-done.5.refs_7_ = bf16[2,16,4096]{2,1,0:T(8,128)(2,1)S(1)} collective-permute-done((bf16[2,16,4096]{2,1,0:T(8,128)(2,1)S(1)}, bf16[2,16,4096]{2,1,0:T(8,128)(2,1)S(1)}, u32[]{:S(2)}, u32[]{:S(2)}) %collective-permute-start.5) | collective-permute-done | bytes 262176 | tf_op jit(solution)/shard_map/ppermute | solution.py:323
  13.9 1.6 %collective-permute-start.6 = (bf16[2,16,4096]{2,1,0:T(8,128)(2,1)S(1)}, bf16[2,16,4096]{2,1,0:T(8,128)(2,1)S(1)}, u32[]{:S(2)}, u32[]{:S(2)}) collective-permute-start(bf16[2,16,4096]{2,1,0:T(8,128)(2,1)S(1)} %broadcast_select_fusion.2), channel_id=1, source_target_pairs={{0,4},{4,0},{8,12},{12,8},{16,20},{20,16},{24,28},{28,24},{1,5},{5... | collective-permute-start | bytes 786440 | tf_op jit(solution)/shard_map/ppermute | solution.py:307
  15.5 1.5 %collective-permute-start.2 = (bf16[2,16,4096]{2,1,0:T(8,128)(2,1)S(1)}, bf16[2,16,4096]{2,1,0:T(8,128)(2,1)S(1)}, u32[]{:S(2)}, u32[]{:S(2)}) collective-permute-start(bf16[2,16,4096]{2,1,0:T(8,128)(2,1)S(1)} %collective-permute-done.refs_1_), channel_id=1, source_target_pairs={{0,2},{1,3},{2,0},{3,1},{4,6},{5,7},{6,4},{7,5},{8,10},{9,11},{10,... | collective-permute-start | bytes 786440 | tf_op jit(solution)/shard_map/ppermute | solution.py:307
  17.0 2.0 %collective-permute-done.7.refs_8_ = bf16[2,16,4096]{2,1,0:T(8,128)(2,1)S(1)} collective-permute-done((bf16[2,16,4096]{2,1,0:T(8,128)(2,1)S(1)}, bf16[2,16,4096]{2,1,0:T(8,128)(2,1)S(1)}, u32[]{:S(2)}, u32[]{:S(2)}) %collective-permute-start.7) | collective-permute-done | bytes 262176 | tf_op jit(solution)/shard_map/ppermute | solution.py:323
  18.9 2.1 %collective-permute-start.12 = (bf16[2,16,4096]{2,1,0:T(8,128)(2,1)S(1)}, bf16[2,16,4096]{2,1,0:T(8,128)(2,1)S(1)}, u32[]{:S(2)}, u32[]{:S(2)}) collective-permute-start(bf16[2,16,4096]{2,1,0:T(8,128)(2,1)S(1)} %collective-permute-done.5.refs_7_), channel_id=1, source_target_pairs={{0,2},{1,3},{2,0},{3,1},{4,6},{5,7},{6,4},{7,5},{8,10},{9,11},{10,... | collective-permute-start | bytes 786440 | tf_op jit(solution)/shard_map/ppermute | solution.py:307
  21.1 2.6 %collective-permute-done.2.refs_3_ = bf16[2,16,4096]{2,1,0:T(8,128)(2,1)S(1)} collective-permute-done((bf16[2,16,4096]{2,1,0:T(8,128)(2,1)S(1)}, bf16[2,16,4096]{2,1,0:T(8,128)(2,1)S(1)}, u32[]{:S(2)}, u32[]{:S(2)}) %collective-permute-start.2) | collective-permute-done | bytes 262176 | tf_op jit(solution)/shard_map/ppermute | solution.py:307
  23.6 0.1 collective-permute-start.8
  23.8 0.0 collective-permute-done.1.refs_2_
  23.8 0.7 collective-permute-start.10
  24.5 0.0 collective-permute-done.6.refs_7_
  24.5 1.3 %collective-permute-start.4 = (bf16[4,16,4096]{2,1,0:T(8,128)(2,1)S(1)}, bf16[4,16,4096]{2,1,0:T(8,128)(2,1)S(1)}, u32[]{:S(2)}, u32[]{:S(2)}) collective-permute-start(bf16[4,16,4096]{2,1,0:T(8,128)(2,1)S(1)} %pad_maximum_fusion), channel_id=1, source_target_pairs={{0,1},{3,2},{4,5},{7,6},{8,9},{11,10},{12,13},{15,14},{16,17},{19,... | collective-permute-start | bytes 1572872 | tf_op jit(solution)/shard_map/ppermute | solution.py:307
  25.8 6.4 %collective-permute-done.10.refs_10_ = bf16[2,16,4096]{2,1,0:T(8,128)(2,1)S(1)} collective-permute-done((bf16[2,16,4096]{2,1,0:T(8,128)(2,1)S(1)}, bf16[2,16,4096]{2,1,0:T(8,128)(2,1)S(1)}, u32[]{:S(2)}, u32[]{:S(2)}) %collective-permute-start.10) | collective-permute-done | bytes 262176 | tf_op jit(solution)/shard_map/ppermute | solution.py:323
  32.2 2.1 %collective-permute-start.9 = (bf16[2,16,4096]{2,1,0:T(8,128)(2,1)S(1)}, bf16[2,16,4096]{2,1,0:T(8,128)(2,1)S(1)}, u32[]{:S(2)}, u32[]{:S(2)}) collective-permute-start(bf16[2,16,4096]{2,1,0:T(8,128)(2,1)S(1)} %collective-permute-done.6.refs_7_), channel_id=1, source_target_pairs={{0,2},{1,3},{2,0},{3,1},{4,6},{5,7},{6,4},{7,5},{8,10},{9,11},{10,... | collective-permute-start | bytes 786440 | tf_op jit(solution)/shard_map/ppermute | solution.py:307
  34.3 0.0 collective-permute-done.3.refs_5_
  34.4 2.1 %collective-permute-start.11 = (bf16[2,16,4096]{2,1,0:T(8,128)(2,1)S(1)}, bf16[2,16,4096]{2,1,0:T(8,128)(2,1)S(1)}, u32[]{:S(2)}, u32[]{:S(2)}) collective-permute-start(bf16[2,16,4096]{2,1,0:T(8,128)(2,1)S(1)} %broadcast_select_fusion), channel_id=1, source_target_pairs={{0,4},{4,0},{8,12},{12,8},{16,20},{20,16},{24,28},{28,24},{1,5},{5... | collective-permute-start | bytes 786440 | tf_op jit(solution)/shard_map/ppermute | solution.py:307
  36.4 0.0 collective-permute-done.12.refs_9_
  36.4 0.0 collective-permute-done.4.refs_6_
  36.4 4.4 %shard_map.31.refs_13_ = f32[2,64,4096]{2,1,0:T(8,128)S(1)} custom-call(bf16[2,16,4096]{2,1,0:T(8,128)(2,1)S(1)} %get-tuple-element.11.refs_0_, bf16[2,16,4096]{2,1,0:T(8,128)(2,1)S(1)} %collective-permute-done.refs_1_, bf16[2,16,4096]{2,1,0:T(8,128)(2,1)S(1)} %collective-permute-done.1.refs_2_, bf16[2,16,4096]{2,1,0:T(8,128)(2,1)S(1)} %collective-permute-done.2.refs_3_, ...), custom_call_target="tpu_custom_call" | custom-call | flops 3221225472 | bytes 8388608 | tf_op jit(solution)/shard_map/pallas_call | solution.py:220
  40.8 0.0 collective-permute-done.8.refs_8_
  40.8 0.0 collective-permute-done.9.refs_9_
  40.9 0.0 collective-permute-done.11.refs_10_
  40.9 4.4 %shard_map.32 = (f32[64,4096]{1,0:T(8,128)S(1)}, bf16[64,4096]{1,0:T(8,128)(2,1)S(1)}) custom-call(bf16[2,16,4096]{2,1,0:T(8,128)(2,1)S(1)} %get-tuple-element.11.refs_0_, bf16[2,16,4096]{2,1,0:T(8,128)(2,1)S(1)} %collective-permute-done.refs_1_, bf16[2,16,4096]{2,1,0:T(8,128)(2,1)S(1)} %collective-permute-done.1.refs_2_, ...), custom_call_target="tpu_custom_call" | custom-call | flops 3221225472 | bytes 8388608 | tf_op jit(solution)/shard_map/pallas_call | solution.py:220
  45.3 0.1 collective-permute-start.13
  45.4 1.9 %collective-permute-done.13.part_ref = bf16[64,4096]{1,0:T(8,128)(2,1)S(1)} collective-permute-done((bf16[64,4096]{1,0:T(8,128)(2,1)S(1)}, bf16[64,4096]{1,0:T(8,128)(2,1)S(1)}, u32[]{:S(2)}, u32[]{:S(2)}) %collective-permute-start.13) | collective-permute-done | bytes 524320 | tf_op jit(solution)/shard_map/ppermute | solution.py:307
  47.3 0.1 shard_map.33
  47.4 17.7 %all_to_all.10.x_ref = bf16[32,16,512]{2,1,0:T(8,128)(2,1)S(1)} all-to-all(bf16[32,16,512]{2,1,0:T(8,128)(2,1)S(1)} %bitcast.1), channel_id=1, replica_groups=mesh['blk'=8,'grid'=4] {'blk','grid'}, dimensions={0} | all-to-all | bytes 1048576 | tf_op jit(solution)/shard_map/all_to_all | solution.py:366
  65.1 0.7 shard_map.34
  65.8 11.0 %all_to_all.11.parts_ref = f32[32,8,128]{2,1,0:T(8,128)S(1)} all-to-all(f32[32,8,128]{2,1,0:T(8,128)S(1)} %shard_map.34), channel_id=1, replica_groups=mesh['blk'=8,'grid'=4] {'blk','grid'}, dimensions={0} | all-to-all | bytes 262144 | tf_op jit(solution)/shard_map/all_to_all | solution.py:378
  76.8 2.4 %shard_map.35 = (bf16[32,16,512]{2,1,0:T(8,128)(2,1)}, f32[32,32]{1,0:T(8,128)}) custom-call(f32[32,8,128]{2,1,0:T(8,128)S(1)} %all_to_all.11.parts_ref, bf16[32,16,512]{2,1,0:T(8,128)(2,1)S(1)} %all_to_all.10.x_ref), custom_call_target="tpu_custom_call" | custom-call | tf_op jit(solution)/shard_map/pallas_call | solution.py:379
  (4 shorter events, 0.1 us)
Async XLA Ops:
  1.7 7.4 %collective-permute-start = (bf16[2,16,4096]{2,1,0:T(8,128)(2,1)S(1)}, bf16[2,16,4096]{2,1,0:T(8,128)(2,1)S(1)}, u32[]{:S(2)}, u32[]{:S(2)}) collective-permute-start(bf16[2,16,4096]{2,1,0:T(8,128)(2,1)S(1)} %get-tuple-element.12.refs_4_), channel_id=1, source_target_pairs={{0,1},{1,0},{2,3},{3,2},{4,5},{5,4},{6,7},{7,6},{8,9},{9,8},{10,11... | collective-permute-start | bytes 786440 | tf_op jit(solution)/shard_map/ppermute | solution.py:307
  2.3 11.6 %collective-permute-start.5 = (bf16[2,16,4096]{2,1,0:T(8,128)(2,1)S(1)}, bf16[2,16,4096]{2,1,0:T(8,128)(2,1)S(1)}, u32[]{:S(2)}, u32[]{:S(2)}) collective-permute-start(bf16[2,16,4096]{2,1,0:T(8,128)(2,1)S(1)} %get-tuple-element.11.refs_0_), channel_id=1, source_target_pairs={{0,8},{4,12},{8,16},{12,20},{16,24},{20,28},{24,0},{28,4},{1,9},{5... | collective-permute-start | bytes 786440 | tf_op jit(solution)/shard_map/ppermute | solution.py:323
  4.9 29.4 %collective-permute-start.3 = (bf16[2,16,4096]{2,1,0:T(8,128)(2,1)S(1)}, bf16[2,16,4096]{2,1,0:T(8,128)(2,1)S(1)}, u32[]{:S(2)}, u32[]{:S(2)}) collective-permute-start(bf16[2,16,4096]{2,1,0:T(8,128)(2,1)S(1)} %get-tuple-element.11.refs_0_), channel_id=1, source_target_pairs={{0,1},{3,2},{4,5},{7,6},{8,9},{11,10},{12,13},{15,14},{16,17},{19,... | collective-permute-start | bytes 786440 | tf_op jit(solution)/shard_map/ppermute | solution.py:307
  7.0 16.8 %collective-permute-start.1 = (bf16[2,16,4096]{2,1,0:T(8,128)(2,1)S(1)}, bf16[2,16,4096]{2,1,0:T(8,128)(2,1)S(1)}, u32[]{:S(2)}, u32[]{:S(2)}) collective-permute-start(bf16[2,16,4096]{2,1,0:T(8,128)(2,1)S(1)} %get-tuple-element.11.refs_0_), channel_id=1, source_target_pairs={{1,3},{2,0},{5,7},{6,4},{9,11},{10,8},{13,15},{14,12},{17,19},{18,... | collective-permute-start | bytes 786440 | tf_op jit(solution)/shard_map/ppermute | solution.py:307
  9.1 9.8 %collective-permute-start.7 = (bf16[2,16,4096]{2,1,0:T(8,128)(2,1)S(1)}, bf16[2,16,4096]{2,1,0:T(8,128)(2,1)S(1)}, u32[]{:S(2)}, u32[]{:S(2)}) collective-permute-start(bf16[2,16,4096]{2,1,0:T(8,128)(2,1)S(1)} %collective-permute-done.refs_1_), channel_id=1, source_target_pairs={{0,8},{4,12},{8,16},{12,20},{16,24},{20,28},{24,0},{28,4},{1,9},{5... | collective-permute-start | bytes 786440 | tf_op jit(solution)/shard_map/ppermute | solution.py:323
  13.9 10.6 %collective-permute-start.6 = (bf16[2,16,4096]{2,1,0:T(8,128)(2,1)S(1)}, bf16[2,16,4096]{2,1,0:T(8,128)(2,1)S(1)}, u32[]{:S(2)}, u32[]{:S(2)}) collective-permute-start(bf16[2,16,4096]{2,1,0:T(8,128)(2,1)S(1)} %broadcast_select_fusion.2), channel_id=1, source_target_pairs={{0,4},{4,0},{8,12},{12,8},{16,20},{20,16},{24,28},{28,24},{1,5},{5... | collective-permute-start | bytes 786440 | tf_op jit(solution)/shard_map/ppermute | solution.py:307
  15.5 8.2 %collective-permute-start.2 = (bf16[2,16,4096]{2,1,0:T(8,128)(2,1)S(1)}, bf16[2,16,4096]{2,1,0:T(8,128)(2,1)S(1)}, u32[]{:S(2)}, u32[]{:S(2)}) collective-permute-start(bf16[2,16,4096]{2,1,0:T(8,128)(2,1)S(1)} %collective-permute-done.refs_1_), channel_id=1, source_target_pairs={{0,2},{1,3},{2,0},{3,1},{4,6},{5,7},{6,4},{7,5},{8,10},{9,11},{10,... | collective-permute-start | bytes 786440 | tf_op jit(solution)/shard_map/ppermute | solution.py:307
  18.9 17.5 %collective-permute-start.12 = (bf16[2,16,4096]{2,1,0:T(8,128)(2,1)S(1)}, bf16[2,16,4096]{2,1,0:T(8,128)(2,1)S(1)}, u32[]{:S(2)}, u32[]{:S(2)}) collective-permute-start(bf16[2,16,4096]{2,1,0:T(8,128)(2,1)S(1)} %collective-permute-done.5.refs_7_), channel_id=1, source_target_pairs={{0,2},{1,3},{2,0},{3,1},{4,6},{5,7},{6,4},{7,5},{8,10},{9,11},{10,... | collective-permute-start | bytes 786440 | tf_op jit(solution)/shard_map/ppermute | solution.py:307
  23.6 17.2 %collective-permute-start.8 = (bf16[2,16,4096]{2,1,0:T(8,128)(2,1)S(1)}, bf16[2,16,4096]{2,1,0:T(8,128)(2,1)S(1)}, u32[]{:S(2)}, u32[]{:S(2)}) collective-permute-start(bf16[2,16,4096]{2,1,0:T(8,128)(2,1)S(1)} %broadcast_select_fusion.1), channel_id=1, source_target_pairs={{0,4},{4,0},{8,12},{12,8},{16,20},{20,16},{24,28},{28,24},{1,5},{5... | collective-permute-start | bytes 786440 | tf_op jit(solution)/shard_map/ppermute | solution.py:307
  23.8 8.5 %collective-permute-start.10 = (bf16[2,16,4096]{2,1,0:T(8,128)(2,1)S(1)}, bf16[2,16,4096]{2,1,0:T(8,128)(2,1)S(1)}, u32[]{:S(2)}, u32[]{:S(2)}) collective-permute-start(bf16[2,16,4096]{2,1,0:T(8,128)(2,1)S(1)} %collective-permute-done.2.refs_3_), channel_id=1, source_target_pairs={{0,8},{4,12},{8,16},{12,20},{16,24},{20,28},{24,0},{28,4},{1,9},{5... | collective-permute-start | bytes 786440 | tf_op jit(solution)/shard_map/ppermute | solution.py:323
  24.5 12.0 %collective-permute-start.4 = (bf16[4,16,4096]{2,1,0:T(8,128)(2,1)S(1)}, bf16[4,16,4096]{2,1,0:T(8,128)(2,1)S(1)}, u32[]{:S(2)}, u32[]{:S(2)}) collective-permute-start(bf16[4,16,4096]{2,1,0:T(8,128)(2,1)S(1)} %pad_maximum_fusion), channel_id=1, source_target_pairs={{0,1},{3,2},{4,5},{7,6},{8,9},{11,10},{12,13},{15,14},{16,17},{19,... | collective-permute-start | bytes 1572872 | tf_op jit(solution)/shard_map/ppermute | solution.py:307
  32.2 8.6 %collective-permute-start.9 = (bf16[2,16,4096]{2,1,0:T(8,128)(2,1)S(1)}, bf16[2,16,4096]{2,1,0:T(8,128)(2,1)S(1)}, u32[]{:S(2)}, u32[]{:S(2)}) collective-permute-start(bf16[2,16,4096]{2,1,0:T(8,128)(2,1)S(1)} %collective-permute-done.6.refs_7_), channel_id=1, source_target_pairs={{0,2},{1,3},{2,0},{3,1},{4,6},{5,7},{6,4},{7,5},{8,10},{9,11},{10,... | collective-permute-start | bytes 786440 | tf_op jit(solution)/shard_map/ppermute | solution.py:307
  34.4 6.5 %collective-permute-start.11 = (bf16[2,16,4096]{2,1,0:T(8,128)(2,1)S(1)}, bf16[2,16,4096]{2,1,0:T(8,128)(2,1)S(1)}, u32[]{:S(2)}, u32[]{:S(2)}) collective-permute-start(bf16[2,16,4096]{2,1,0:T(8,128)(2,1)S(1)} %broadcast_select_fusion), channel_id=1, source_target_pairs={{0,4},{4,0},{8,12},{12,8},{16,20},{20,16},{24,28},{28,24},{1,5},{5... | collective-permute-start | bytes 786440 | tf_op jit(solution)/shard_map/ppermute | solution.py:307
  45.3 2.0 %collective-permute-start.13 = (bf16[64,4096]{1,0:T(8,128)(2,1)S(1)}, bf16[64,4096]{1,0:T(8,128)(2,1)S(1)}, u32[]{:S(2)}, u32[]{:S(2)}) collective-permute-start(bf16[64,4096]{1,0:T(8,128)(2,1)S(1)} %get-tuple-element.19), channel_id=1, source_target_pairs={{0,1},{1,0},{2,3},{3,2},{4,5},{5,4},{6,7},{7,6},{8,9},{9,8},{10,11... | collective-permute-start | bytes 1572872 | tf_op jit(solution)/shard_map/ppermute | solution.py:307

commit v3 on v1

--- a/solution.py
+++ b/solution.py
@@ -24,7 +24,7 @@
 ROW_PAD = 1
 SMALL_VMEM = 10 * 1024 * 1024
 QUAD = 4
-PANEL = 8
+PANEL = 4
 
 
 def product(a, b):
@@ -341,7 +341,8 @@
     tables = (diagonals, weights)
     near_other = [exchanged(near[0], "grid", top), relayed(relay, far_other[1])]
     local = held + across
-    passed = [give, passed_on(held[0]), passed_on(jnp.concatenate([across[1], across[0]], 0))]
+    joined = jnp.concatenate([across[1], across[0]], 0)
+    passed = [give, passed_on(held[0]), passed_on(joined)]
     acc = add_block(local, passed, far + far_other, tables, None)
     mine, other = add_block(local, passed, near + near_other, tables, acc)
     other = exchanged(other, "grid", 1)

time: 79.1 us -> 79.6 us (level)
  no operation moved by 1% of the time
where the time goes in v3:
time: 79.6 us; the launch traced here: 79.4 us
  blocking collectives  28.7 us (36%)
  starting transfers between devices  18.7 us (23%)
  waiting for transfers between devices  16.7 us (21%)
  Pallas kernels  13.3 us (17%)
  local copies, waits for them, and re-layouts  1.07 us (1%)
    all_to_all x1, blocking collectives, body(): cellwise = lax.all_to_all(updated, ('blk', 'grid'), 0, 0, tiled=True)  17.7 us
    ppermute x11, starting transfers between devices, exchanged(): lax.ppermute(x, axis, [(i, i ^ by) for i in range(lax.axis_size(axis)) if...  13.7 us
    ppermute x3, waiting for transfers between devices, shifted(): lax.ppermute(x, 'blk', [(i, (i + 2) % blocks) for i in range(blocks)])  11.8 us
    all_to_all x1, blocking collectives, body(): parts = lax.all_to_all(local, ('blk', 'grid'), 0, 0, tiled=True)  11 us
    pallas_call x2, Pallas kernels, add_block(): pl.pallas_call(lambda *refs: block_kernel(counts, final, refs), out_shape...  8.8 us
    ppermute x3, starting transfers between devices, shifted(): lax.ppermute(x, 'blk', [(i, (i + 2) % blocks) for i in range(blocks)])  5.01 us
    ppermute x11, waiting for transfers between devices, exchanged(): lax.ppermute(x, axis, [(i, i ^ by) for i in range(lax.axis_size(axis)) if...  4.93 us
    pallas_call x1, Pallas kernels, body(): pl.pallas_call(functools.partial(rotate_kernel, 1.0 / cell_count), out_sh...  2.86 us
  transfers between devices with their start and end apart: 14, of which 5 were waited for; matrix products, arithmetic and copies ran while one was open for 0% of the time, Pallas kernels for 7%

profile of v3, /device:TPU:0, one launch (start us, length us, event | category | flops | bytes accessed | tf_op | source)
XLA Modules:
  0.0 79.4 jit_solution(17225318269150455015)
XLA Ops:
  0.6 1.1 %constant_dynamic-slice_fusion = (bf16[2,16,4096]{2,1,0:T(8,128)(2,1)S(1)}, bf16[2,16,4096]{2,1,0:T(8,128)(2,1)S(1)}) fusion(bf16[4,16,4096]{2,1,0:T(8,128)(2,1)} %param.1, s32[]{:T(128)S(6)} %select_n.35, s32[]{:T(128)S(6)} %select_n.34), kind=kLoop, calls=%fused_computation.4 | loop fusion | bytes 1048584 | tf_op jit(solution)/shard_map/dynamic_slice | solution.py:333
  1.7 0.6 collective-permute-start
  2.3 2.6 %collective-permute-start.5 = (bf16[2,16,4096]{2,1,0:T(8,128)(2,1)S(1)}, bf16[2,16,4096]{2,1,0:T(8,128)(2,1)S(1)}, u32[]{:S(2)}, u32[]{:S(2)}) collective-permute-start(bf16[2,16,4096]{2,1,0:T(8,128)(2,1)S(1)} %get-tuple-element.11.refs_0_), channel_id=1, source_target_pairs={{0,8},{4,12},{8,16},{12,20},{16,24},{20,28},{24,0},{28,4},{1,9},{5... | collective-permute-start | bytes 786440 | tf_op jit(solution)/shard_map/ppermute | solution.py:323
  4.9 2.1 %collective-permute-start.3 = (bf16[2,16,4096]{2,1,0:T(8,128)(2,1)S(1)}, bf16[2,16,4096]{2,1,0:T(8,128)(2,1)S(1)}, u32[]{:S(2)}, u32[]{:S(2)}) collective-permute-start(bf16[2,16,4096]{2,1,0:T(8,128)(2,1)S(1)} %get-tuple-element.11.refs_0_), channel_id=1, source_target_pairs={{0,1},{3,2},{4,5},{7,6},{8,9},{11,10},{12,13},{15,14},{16,17},{19,... | collective-permute-start | bytes 786440 | tf_op jit(solution)/shard_map/ppermute | solution.py:307
  7.0 0.8 collective-permute-start.1
  7.8 0.8 %shard_map.30 = (bf16[4,256,256]{2,1,0:T(8,128)(2,1)S(1)}, f32[4096,128]{1,0:T(8,128)S(1)}) custom-call(), custom_call_target="tpu_custom_call" | custom-call | flops 268435456 | bytes 3145728 | tf_op jit(solution)/shard_map/pallas_call | solution.py:83
  8.6 0.0 collective-permute-done.refs_1_
  8.6 1.6 %collective-permute-start.7 = (bf16[2,16,4096]{2,1,0:T(8,128)(2,1)S(1)}, bf16[2,16,4096]{2,1,0:T(8,128)(2,1)S(1)}, u32[]{:S(2)}, u32[]{:S(2)}) collective-permute-start(bf16[2,16,4096]{2,1,0:T(8,128)(2,1)S(1)} %collective-permute-done.refs_1_), channel_id=1, source_target_pairs={{0,8},{4,12},{8,16},{12,20},{16,24},{20,28},{24,0},{28,4},{1,9},{5... | collective-permute-start | bytes 786440 | tf_op jit(solution)/shard_map/ppermute | solution.py:323
  10.2 3.6 %collective-permute-done.5.refs_7_ = bf16[2,16,4096]{2,1,0:T(8,128)(2,1)S(1)} collective-permute-done((bf16[2,16,4096]{2,1,0:T(8,128)(2,1)S(1)}, bf16[2,16,4096]{2,1,0:T(8,128)(2,1)S(1)}, u32[]{:S(2)}, u32[]{:S(2)}) %collective-permute-start.5) | collective-permute-done | bytes 262176 | tf_op jit(solution)/shard_map/ppermute | solution.py:323
  13.9 1.6 %collective-permute-start.6 = (bf16[2,16,4096]{2,1,0:T(8,128)(2,1)S(1)}, bf16[2,16,4096]{2,1,0:T(8,128)(2,1)S(1)}, u32[]{:S(2)}, u32[]{:S(2)}) collective-permute-start(bf16[2,16,4096]{2,1,0:T(8,128)(2,1)S(1)} %broadcast_select_fusion.2), channel_id=1, source_target_pairs={{0,4},{4,0},{8,12},{12,8},{16,20},{20,16},{24,28},{28,24},{1,5},{5... | collective-permute-start | bytes 786440 | tf_op jit(solution)/shard_map/ppermute | solution.py:307
  15.5 2.0 %collective-permute-start.2 = (bf16[2,16,4096]{2,1,0:T(8,128)(2,1)S(1)}, bf16[2,16,4096]{2,1,0:T(8,128)(2,1)S(1)}, u32[]{:S(2)}, u32[]{:S(2)}) collective-permute-start(bf16[2,16,4096]{2,1,0:T(8,128)(2,1)S(1)} %collective-permute-done.refs_1_), channel_id=1, source_target_pairs={{0,2},{1,3},{2,0},{3,1},{4,6},{5,7},{6,4},{7,5},{8,10},{9,11},{10,... | collective-permute-start | bytes 786440 | tf_op jit(solution)/shard_map/ppermute | solution.py:307
  17.4 2.1 %collective-permute-done.7.refs_8_ = bf16[2,16,4096]{2,1,0:T(8,128)(2,1)S(1)} collective-permute-done((bf16[2,16,4096]{2,1,0:T(8,128)(2,1)S(1)}, bf16[2,16,4096]{2,1,0:T(8,128)(2,1)S(1)}, u32[]{:S(2)}, u32[]{:S(2)}) %collective-permute-start.7) | collective-permute-done | bytes 262176 | tf_op jit(solution)/shard_map/ppermute | solution.py:323
  19.5 1.5 %collective-permute-start.12 = (bf16[2,16,4096]{2,1,0:T(8,128)(2,1)S(1)}, bf16[2,16,4096]{2,1,0:T(8,128)(2,1)S(1)}, u32[]{:S(2)}, u32[]{:S(2)}) collective-permute-start(bf16[2,16,4096]{2,1,0:T(8,128)(2,1)S(1)} %collective-permute-done.5.refs_7_), channel_id=1, source_target_pairs={{0,2},{1,3},{2,0},{3,1},{4,6},{5,7},{6,4},{7,5},{8,10},{9,11},{10,... | collective-permute-start | bytes 786440 | tf_op jit(solution)/shard_map/ppermute | solution.py:307
  21.0 3.0 %collective-permute-done.2.refs_3_ = bf16[2,16,4096]{2,1,0:T(8,128)(2,1)S(1)} collective-permute-done((bf16[2,16,4096]{2,1,0:T(8,128)(2,1)S(1)}, bf16[2,16,4096]{2,1,0:T(8,128)(2,1)S(1)}, u32[]{:S(2)}, u32[]{:S(2)}) %collective-permute-start.2) | collective-permute-done | bytes 262176 | tf_op jit(solution)/shard_map/ppermute | solution.py:307
  24.0 0.0 collective-permute-start.8
  24.0 0.0 collective-permute-done.1.refs_2_
  24.0 0.8 collective-permute-start.10
  24.8 0.0 collective-permute-done.6.refs_7_
  24.8 1.3 %collective-permute-start.4 = (bf16[4,16,4096]{2,1,0:T(8,128)(2,1)S(1)}, bf16[4,16,4096]{2,1,0:T(8,128)(2,1)S(1)}, u32[]{:S(2)}, u32[]{:S(2)}) collective-permute-start(bf16[4,16,4096]{2,1,0:T(8,128)(2,1)S(1)} %pad_maximum_fusion), channel_id=1, source_target_pairs={{0,1},{3,2},{4,5},{7,6},{8,9},{11,10},{12,13},{15,14},{16,17},{19,... | collective-permute-start | bytes 1572872 | tf_op jit(solution)/shard_map/ppermute | solution.py:307
  26.2 6.1 %collective-permute-done.10.refs_10_ = bf16[2,16,4096]{2,1,0:T(8,128)(2,1)S(1)} collective-permute-done((bf16[2,16,4096]{2,1,0:T(8,128)(2,1)S(1)}, bf16[2,16,4096]{2,1,0:T(8,128)(2,1)S(1)}, u32[]{:S(2)}, u32[]{:S(2)}) %collective-permute-start.10) | collective-permute-done | bytes 262176 | tf_op jit(solution)/shard_map/ppermute | solution.py:323
  32.2 1.8 %collective-permute-start.9 = (bf16[2,16,4096]{2,1,0:T(8,128)(2,1)S(1)}, bf16[2,16,4096]{2,1,0:T(8,128)(2,1)S(1)}, u32[]{:S(2)}, u32[]{:S(2)}) collective-permute-start(bf16[2,16,4096]{2,1,0:T(8,128)(2,1)S(1)} %collective-permute-done.6.refs_7_), channel_id=1, source_target_pairs={{0,2},{1,3},{2,0},{3,1},{4,6},{5,7},{6,4},{7,5},{8,10},{9,11},{10,... | collective-permute-start | bytes 786440 | tf_op jit(solution)/shard_map/ppermute | solution.py:307
  34.1 0.0 collective-permute-done.3.refs_5_
  34.1 2.1 %collective-permute-start.11 = (bf16[2,16,4096]{2,1,0:T(8,128)(2,1)S(1)}, bf16[2,16,4096]{2,1,0:T(8,128)(2,1)S(1)}, u32[]{:S(2)}, u32[]{:S(2)}) collective-permute-start(bf16[2,16,4096]{2,1,0:T(8,128)(2,1)S(1)} %broadcast_select_fusion), channel_id=1, source_target_pairs={{0,4},{4,0},{8,12},{12,8},{16,20},{20,16},{24,28},{28,24},{1,5},{5... | collective-permute-start | bytes 786440 | tf_op jit(solution)/shard_map/ppermute | solution.py:307
  36.2 0.0 collective-permute-done.12.refs_9_
  36.2 0.0 collective-permute-done.4.refs_6_
  36.2 4.4 %shard_map.31.refs_13_ = f32[2,64,4096]{2,1,0:T(8,128)S(1)} custom-call(bf16[2,16,4096]{2,1,0:T(8,128)(2,1)S(1)} %get-tuple-element.11.refs_0_, bf16[2,16,4096]{2,1,0:T(8,128)(2,1)S(1)} %collective-permute-done.refs_1_, bf16[2,16,4096]{2,1,0:T(8,128)(2,1)S(1)} %collective-permute-done.1.refs_2_, bf16[2,16,4096]{2,1,0:T(8,128)(2,1)S(1)} %collective-permute-done.2.refs_3_, ...), custom_call_target="tpu_custom_call" | custom-call | flops 3221225472 | bytes 8388608 | tf_op jit(solution)/shard_map/pallas_call | solution.py:220
  40.6 0.0 collective-permute-done.8.refs_8_
  40.6 0.0 collective-permute-done.9.refs_9_
  40.6 0.0 collective-permute-done.11.refs_10_
  40.6 4.4 %shard_map.32 = (f32[64,4096]{1,0:T(8,128)S(1)}, bf16[64,4096]{1,0:T(8,128)(2,1)S(1)}) custom-call(bf16[2,16,4096]{2,1,0:T(8,128)(2,1)S(1)} %get-tuple-element.11.refs_0_, bf16[2,16,4096]{2,1,0:T(8,128)(2,1)S(1)} %collective-permute-done.refs_1_, bf16[2,16,4096]{2,1,0:T(8,128)(2,1)S(1)} %collective-permute-done.1.refs_2_, ...), custom_call_target="tpu_custom_call" | custom-call | flops 3221225472 | bytes 8388608 | tf_op jit(solution)/shard_map/pallas_call | solution.py:220
  45.0 0.1 collective-permute-start.13
  45.1 1.9 %collective-permute-done.13.part_ref = bf16[64,4096]{1,0:T(8,128)(2,1)S(1)} collective-permute-done((bf16[64,4096]{1,0:T(8,128)(2,1)S(1)}, bf16[64,4096]{1,0:T(8,128)(2,1)S(1)}, u32[]{:S(2)}, u32[]{:S(2)}) %collective-permute-start.13) | collective-permute-done | bytes 524320 | tf_op jit(solution)/shard_map/ppermute | solution.py:307
  47.0 0.1 shard_map.33
  47.1 17.7 %all_to_all.10.x_ref = bf16[32,16,512]{2,1,0:T(8,128)(2,1)S(1)} all-to-all(bf16[32,16,512]{2,1,0:T(8,128)(2,1)S(1)} %bitcast.1), channel_id=1, replica_groups=mesh['blk'=8,'grid'=4] {'blk','grid'}, dimensions={0} | all-to-all | bytes 1048576 | tf_op jit(solution)/shard_map/all_to_all | solution.py:364
  64.8 0.7 shard_map.34
  65.5 11.0 %all_to_all.11.parts_ref = f32[32,8,128]{2,1,0:T(8,128)S(1)} all-to-all(f32[32,8,128]{2,1,0:T(8,128)S(1)} %shard_map.34), channel_id=1, replica_groups=mesh['blk'=8,'grid'=4] {'blk','grid'}, dimensions={0} | all-to-all | bytes 262144 | tf_op jit(solution)/shard_map/all_to_all | solution.py:376
  76.5 2.9 %shard_map.35 = (bf16[32,16,512]{2,1,0:T(8,128)(2,1)}, f32[32,32]{1,0:T(8,128)}) custom-call(f32[32,8,128]{2,1,0:T(8,128)S(1)} %all_to_all.11.parts_ref, bf16[32,16,512]{2,1,0:T(8,128)(2,1)S(1)} %all_to_all.10.x_ref), custom_call_target="tpu_custom_call" | custom-call | tf_op jit(solution)/shard_map/pallas_call | solution.py:377
  (4 shorter events, 0.1 us)
Async XLA Ops:
  1.7 6.8 %collective-permute-start = (bf16[2,16,4096]{2,1,0:T(8,128)(2,1)S(1)}, bf16[2,16,4096]{2,1,0:T(8,128)(2,1)S(1)}, u32[]{:S(2)}, u32[]{:S(2)}) collective-permute-start(bf16[2,16,4096]{2,1,0:T(8,128)(2,1)S(1)} %get-tuple-element.12.refs_4_), channel_id=1, source_target_pairs={{0,1},{1,0},{2,3},{3,2},{4,5},{5,4},{6,7},{7,6},{8,9},{9,8},{10,11... | collective-permute-start | bytes 786440 | tf_op jit(solution)/shard_map/ppermute | solution.py:307
  2.3 11.6 %collective-permute-start.5 = (bf16[2,16,4096]{2,1,0:T(8,128)(2,1)S(1)}, bf16[2,16,4096]{2,1,0:T(8,128)(2,1)S(1)}, u32[]{:S(2)}, u32[]{:S(2)}) collective-permute-start(bf16[2,16,4096]{2,1,0:T(8,128)(2,1)S(1)} %get-tuple-element.11.refs_0_), channel_id=1, source_target_pairs={{0,8},{4,12},{8,16},{12,20},{16,24},{20,28},{24,0},{28,4},{1,9},{5... | collective-permute-start | bytes 786440 | tf_op jit(solution)/shard_map/ppermute | solution.py:323
  4.9 29.2 %collective-permute-start.3 = (bf16[2,16,4096]{2,1,0:T(8,128)(2,1)S(1)}, bf16[2,16,4096]{2,1,0:T(8,128)(2,1)S(1)}, u32[]{:S(2)}, u32[]{:S(2)}) collective-permute-start(bf16[2,16,4096]{2,1,0:T(8,128)(2,1)S(1)} %get-tuple-element.11.refs_0_), channel_id=1, source_target_pairs={{0,1},{3,2},{4,5},{7,6},{8,9},{11,10},{12,13},{15,14},{16,17},{19,... | collective-permute-start | bytes 786440 | tf_op jit(solution)/shard_map/ppermute | solution.py:307
  7.0 17.0 %collective-permute-start.1 = (bf16[2,16,4096]{2,1,0:T(8,128)(2,1)S(1)}, bf16[2,16,4096]{2,1,0:T(8,128)(2,1)S(1)}, u32[]{:S(2)}, u32[]{:S(2)}) collective-permute-start(bf16[2,16,4096]{2,1,0:T(8,128)(2,1)S(1)} %get-tuple-element.11.refs_0_), channel_id=1, source_target_pairs={{0,2},{1,3},{2,0},{3,1},{4,6},{5,7},{6,4},{7,5},{8,10},{9,11},{10,... | collective-permute-start | bytes 786440 | tf_op jit(solution)/shard_map/ppermute | solution.py:307
  8.6 10.9 %collective-permute-start.7 = (bf16[2,16,4096]{2,1,0:T(8,128)(2,1)S(1)}, bf16[2,16,4096]{2,1,0:T(8,128)(2,1)S(1)}, u32[]{:S(2)}, u32[]{:S(2)}) collective-permute-start(bf16[2,16,4096]{2,1,0:T(8,128)(2,1)S(1)} %collective-permute-done.refs_1_), channel_id=1, source_target_pairs={{0,8},{4,12},{8,16},{12,20},{16,24},{20,28},{24,0},{28,4},{1,9},{5... | collective-permute-start | bytes 786440 | tf_op jit(solution)/shard_map/ppermute | solution.py:323
  13.9 10.9 %collective-permute-start.6 = (bf16[2,16,4096]{2,1,0:T(8,128)(2,1)S(1)}, bf16[2,16,4096]{2,1,0:T(8,128)(2,1)S(1)}, u32[]{:S(2)}, u32[]{:S(2)}) collective-permute-start(bf16[2,16,4096]{2,1,0:T(8,128)(2,1)S(1)} %broadcast_select_fusion.2), channel_id=1, source_target_pairs={{0,4},{4,0},{8,12},{12,8},{16,20},{20,16},{24,28},{28,24},{1,5},{5... | collective-permute-start | bytes 786440 | tf_op jit(solution)/shard_map/ppermute | solution.py:307
  15.5 8.5 %collective-permute-start.2 = (bf16[2,16,4096]{2,1,0:T(8,128)(2,1)S(1)}, bf16[2,16,4096]{2,1,0:T(8,128)(2,1)S(1)}, u32[]{:S(2)}, u32[]{:S(2)}) collective-permute-start(bf16[2,16,4096]{2,1,0:T(8,128)(2,1)S(1)} %collective-permute-done.refs_1_), channel_id=1, source_target_pairs={{0,2},{1,3},{2,0},{3,1},{4,6},{5,7},{6,4},{7,5},{8,10},{9,11},{10,... | collective-permute-start | bytes 786440 | tf_op jit(solution)/shard_map/ppermute | solution.py:307
  19.5 16.7 %collective-permute-start.12 = (bf16[2,16,4096]{2,1,0:T(8,128)(2,1)S(1)}, bf16[2,16,4096]{2,1,0:T(8,128)(2,1)S(1)}, u32[]{:S(2)}, u32[]{:S(2)}) collective-permute-start(bf16[2,16,4096]{2,1,0:T(8,128)(2,1)S(1)} %collective-permute-done.5.refs_7_), channel_id=1, source_target_pairs={{0,2},{1,3},{2,0},{3,1},{4,6},{5,7},{6,4},{7,5},{8,10},{9,11},{10,... | collective-permute-start | bytes 786440 | tf_op jit(solution)/shard_map/ppermute | solution.py:307
  24.0 16.6 %collective-permute-start.8 = (bf16[2,16,4096]{2,1,0:T(8,128)(2,1)S(1)}, bf16[2,16,4096]{2,1,0:T(8,128)(2,1)S(1)}, u32[]{:S(2)}, u32[]{:S(2)}) collective-permute-start(bf16[2,16,4096]{2,1,0:T(8,128)(2,1)S(1)} %broadcast_select_fusion.1), channel_id=1, source_target_pairs={{0,4},{4,0},{8,12},{12,8},{16,20},{20,16},{24,28},{28,24},{1,5},{5... | collective-permute-start | bytes 786440 | tf_op jit(solution)/shard_map/ppermute | solution.py:307
  24.0 8.2 %collective-permute-start.10 = (bf16[2,16,4096]{2,1,0:T(8,128)(2,1)S(1)}, bf16[2,16,4096]{2,1,0:T(8,128)(2,1)S(1)}, u32[]{:S(2)}, u32[]{:S(2)}) collective-permute-start(bf16[2,16,4096]{2,1,0:T(8,128)(2,1)S(1)} %collective-permute-done.2.refs_3_), channel_id=1, source_target_pairs={{0,8},{4,12},{8,16},{12,20},{16,24},{20,28},{24,0},{28,4},{1,9},{5... | collective-permute-start | bytes 786440 | tf_op jit(solution)/shard_map/ppermute | solution.py:323
  24.8 11.4 %collective-permute-start.4 = (bf16[4,16,4096]{2,1,0:T(8,128)(2,1)S(1)}, bf16[4,16,4096]{2,1,0:T(8,128)(2,1)S(1)}, u32[]{:S(2)}, u32[]{:S(2)}) collective-permute-start(bf16[4,16,4096]{2,1,0:T(8,128)(2,1)S(1)} %pad_maximum_fusion), channel_id=1, source_target_pairs={{0,1},{3,2},{4,5},{7,6},{8,9},{11,10},{12,13},{15,14},{16,17},{19,... | collective-permute-start | bytes 1572872 | tf_op jit(solution)/shard_map/ppermute | solution.py:307
  32.2 8.4 %collective-permute-start.9 = (bf16[2,16,4096]{2,1,0:T(8,128)(2,1)S(1)}, bf16[2,16,4096]{2,1,0:T(8,128)(2,1)S(1)}, u32[]{:S(2)}, u32[]{:S(2)}) collective-permute-start(bf16[2,16,4096]{2,1,0:T(8,128)(2,1)S(1)} %collective-permute-done.6.refs_7_), channel_id=1, source_target_pairs={{0,2},{1,3},{2,0},{3,1},{4,6},{5,7},{6,4},{7,5},{8,10},{9,11},{10,... | collective-permute-start | bytes 786440 | tf_op jit(solution)/shard_map/ppermute | solution.py:307
  34.1 6.5 %collective-permute-start.11 = (bf16[2,16,4096]{2,1,0:T(8,128)(2,1)S(1)}, bf16[2,16,4096]{2,1,0:T(8,128)(2,1)S(1)}, u32[]{:S(2)}, u32[]{:S(2)}) collective-permute-start(bf16[2,16,4096]{2,1,0:T(8,128)(2,1)S(1)} %broadcast_select_fusion), channel_id=1, source_target_pairs={{0,4},{4,0},{8,12},{12,8},{16,20},{20,16},{24,28},{28,24},{1,5},{5... | collective-permute-start | bytes 786440 | tf_op jit(solution)/shard_map/ppermute | solution.py:307
  45.0 2.0 %collective-permute-start.13 = (bf16[64,4096]{1,0:T(8,128)(2,1)S(1)}, bf16[64,4096]{1,0:T(8,128)(2,1)S(1)}, u32[]{:S(2)}, u32[]{:S(2)}) collective-permute-start(bf16[64,4096]{1,0:T(8,128)(2,1)S(1)} %get-tuple-element.19), channel_id=1, source_target_pairs={{0,1},{1,0},{2,3},{3,2},{4,5},{5,4},{6,7},{7,6},{8,9},{9,8},{10,11... | collective-permute-start | bytes 1572872 | tf_op jit(solution)/shard_map/ppermute | solution.py:307
